TPU v7x, 32 devices: a whole 2x2x4 slice. The times are simulated.
32 devices in a mesh: leaf: 8 (over z, y), grp: 4 (over x, core).
Axes of the slice: x: 2, y: 2, z: 4, core: 2. Of those that a mesh axis runs over, the one named last changes fastest.
Arguments:
- points: bfloat16 [32768, 256], P(('leaf', 'grp')), may hold values from -0.75 to 0.75
- rhs: float32 [32768, 128], P(('leaf', 'grp')), may hold values from -0.8 to 0.8
- permutation: int32 [32768], P(('leaf', 'grp')), may hold values from 0 to 32767, as said below
- leaf_basis: float32 [8192, 1024], P(('leaf', 'grp')), may hold values from -0.1875 to 0.1875
- climb_leaf: float32 [8192, 256], P(('leaf', 'grp')), may hold values from -0.25 to 0.25
- climb_pair: float32 [4096, 256], P(('leaf', 'grp')), may hold values from -0.25 to 0.25
- climb_quad: float32 [2048, 256], P(('leaf', 'grp')), may hold values from -0.25 to 0.25
- skel_points: bfloat16 [1024, 256], P(('leaf', 'grp')), may hold values from -0.75 to 0.75
- near_lists: int32 [32, 8], replicated, may hold values from -1 to 31, as said below
- far_lists: int32 [4, 3], replicated, may hold values from -1 to 3, as said below
Outputs:
- product: float32 [32768, 128], P(('leaf', 'grp'))
Inputs may be any that keep to these rules, and one draw needn't show every extreme that they name: `permutation`: maps each block of 1024 tree positions of one leaf onto the same block of initial indices, each once. `near_lists`: row t starts with t itself, then distinct other leaves of the same aligned block of eight (t // 8), then -1 entries only; some row has 8 leaves. `far_lists`: row m holds one or more distinct nodes other than m first, then -1 entries only; some row has 3 nodes.
All inputs are finite; a program needn't handle non-finite values.
Results may differ from a plain program's by a relative error of at most 0.0003.
Values may be sent and summed in bfloat16 or wider, within the bound.
No kernel may reach another device: no remote copies, remote signals or barrier semaphores. Data moves between devices by JAX's collectives and lax.ppermute only.
A program may use at most 128 MiB of HBM per device.

v0:
```python
import functools

import jax
import jax.numpy as jnp
from jax import lax
from jax.experimental import pallas as pl
from jax.experimental.pallas import tpu as pltpu
from jax.sharding import PartitionSpec as P


AXES = ("leaf", "grp")
NODE = 8
TINY = 1e-30
SERIES = (
    1.0000005285886142,
    -5.669123056911696e-05,
    -0.4990002868296516,
    0.20543817481505877,
    -0.10204939882030772,
    0.040449241962581796,
    -0.008162324706047165,
)
F32 = jnp.float32
BF16 = jnp.bfloat16
HIGHEST = lax.Precision.HIGHEST
VMEM = pltpu.VMEM
SMEM = pltpu.SMEM


def across(value, mask):
    pairs = [(s, s ^ mask) for s in range(lax.axis_size(AXES))]
    return lax.ppermute(value, AXES, pairs)


def call(kernel, out, n_smem, operands, scratch=(), flops=0, aliases=None):
    specs = [pl.BlockSpec(memory_space=SMEM)] * n_smem
    specs += [pl.BlockSpec(memory_space=VMEM)] * (len(operands) - n_smem)
    multi = isinstance(out, (list, tuple))
    return pl.pallas_call(
        kernel,
        out_shape=out,
        in_specs=specs,
        out_specs=[pl.BlockSpec(memory_space=VMEM)] * len(out)
        if multi
        else pl.BlockSpec(memory_space=VMEM),
        scratch_shapes=list(scratch),
        cost_estimate=pl.CostEstimate(flops=flops, bytes_accessed=0, transcendentals=0),
        compiler_params=pltpu.CompilerParams(vmem_limit_bytes=40 * 2**20),
        input_output_aliases=aliases or {},
    )(*operands)


def halves(value):
    hi = value.astype(BF16)
    return hi, (value - hi.astype(F32)).astype(BF16)


def dot(a, b, dims=((1,), (0,))):
    return lax.dot_general(a, b, (dims, ((), ())), preferred_element_type=F32)


def fine(a, b, dims=((1,), (0,))):
    return lax.dot_general(
        a, b, (dims, ((), ())), precision=HIGHEST, preferred_element_type=F32
    )


def unit_kernel(cosine):
    z = jnp.maximum(1.0 - cosine * cosine, TINY)
    w = z * lax.rsqrt(z)
    acc = jnp.full_like(w, SERIES[-1])
    for coef in SERIES[-2::-1]:
        acc = acc * w + coef
    return acc + cosine


def norms(x):
    x = x.astype(F32)
    sq = jnp.maximum(jnp.sum(x * x, axis=1, keepdims=True), TINY)
    inv = lax.rsqrt(sq)
    return sq * inv, inv


def pack_kernel(x_ref, w_ref, a_ref, b_ref):
    half = x_ref.shape[0] // 2
    width = w_ref.shape[1]
    feats = x_ref.shape[1]
    for k, ref in enumerate((a_ref, b_ref)):
        rows = pl.ds(k * half, half)
        x = x_ref[rows, :]
        ref[0:half, 0:feats] = x
        xf = x.astype(F32)
        length, _ = norms(x)
        hi, lo = halves(w_ref[rows, :] * (length * 0.5))
        ref[0:half, feats : feats + width] = hi
        ref[0:half, feats + width : feats + 2 * width] = lo
        row = fine(jnp.ones((8, feats), F32), xf * xf, ((1,), (1,)))
        inv = lax.rsqrt(jnp.maximum(row, TINY))
        p0 = inv.astype(BF16)
        rest = inv - p0.astype(F32)
        p1 = rest.astype(BF16)
        p2 = (rest - p1.astype(F32)).astype(BF16)
        wide = jnp.zeros((8, ref.shape[1] - half), BF16)
        if wide.shape[1]:
            p0, p1, p2 = (jnp.concatenate([p, wide], 1) for p in (p0, p1, p2))
        ref[half : half + 8, :] = p0
        ref[half + 8 : half + 16, :] = p1
        ref[half + 16 : half + 24, :] = p2
        ref[half + 24 : half + 32, :] = jnp.zeros_like(p0)


def listed(lists_ref, row, value):
    hit = lists_ref[row, 0] == value
    for s in range(1, lists_ref.shape[1]):
        hit = jnp.logical_or(hit, lists_ref[row, s] == value)
    return hit


def near_kernel(masks, first, last, *refs):
    count = len(masks)
    flat_ref, lists_ref, own_ref, mate_ref = refs[:4]
    packs = refs[4 : 4 + count]
    x_ref, p_ref, n_ref, acc_ref, todo_ref = refs[-5:]
    outs = refs[-5 - (2 if last else 1) : -5]
    flat = flat_ref[0]
    size, feats = own_ref.shape
    half = size // 2
    width = acc_ref.shape[2]
    tile = 128
    x_ref[0] = own_ref[...]
    x_ref[1] = mate_ref[...]
    for k, pack in enumerate(packs):
        p_ref[k] = pack[...]
    acc_ref[...] = jnp.zeros_like(acc_ref) if first else refs[4 + count][...]
    for t in range(2):
        for k, mask in enumerate(masks):
            hit = listed(lists_ref, flat ^ t, flat ^ mask)
            todo_ref[t * count + k] = hit.astype(jnp.int32)

    def job(index, carry):
        t = index // count
        k = index % count

        @pl.when(jnp.logical_and(todo_ref[index] > 0, carry != t))
        def _():
            for i in range(size // 256):
                at = pl.ds(i * 256, 256)
                length, inv = norms(x_ref[t, at, :])
                n_ref[0, at, :] = length
                n_ref[1, at, :] = inv

        @pl.when(todo_ref[index] > 0)
        def _():
            inv_row = (
                p_ref[k, half : half + 8, 0:half].astype(F32)
                + p_ref[k, half + 8 : half + 16, 0:half].astype(F32)
                + p_ref[k, half + 16 : half + 24, 0:half].astype(F32)
            )[0:1, :]
            weights = p_ref[k, 0:half, feats : feats + 2 * width]
            for i in range(size // tile):
                at = pl.ds(i * tile, tile)
                c = dot(x_ref[t, at, :], p_ref[k, 0:half, 0:feats], ((1,), (1,)))
                hi, lo = halves(unit_kernel(c * n_ref[1, at, :] * inv_row))
                total = dot(hi, weights) + dot(lo, weights)
                acc_ref[t, at, :] += n_ref[0, at, :] * (total[:, 0:width] + total[:, width:])

        return jnp.where(todo_ref[index] > 0, t, carry)

    lax.fori_loop(0, 2 * count, job, -1)
    if last:
        outs[0][...] = acc_ref[0]
        outs[1][...] = acc_ref[1]
    else:
        outs[0][...] = acc_ref[...]


def basis_kernel(perm_ref, basis_ref, w_ref, first_ref, turned_ref, part_ref, hot_ref):
    size = basis_ref.shape[1]
    rank = basis_ref.shape[0]
    width = w_ref.shape[1]
    place = lax.rem(perm_ref[...], size)
    for i in range(size // 256):
        spot = lax.broadcasted_iota(jnp.int32, (256, size), 0) + i * 256
        hot_ref[i * 256 : (i + 1) * 256, :] = jnp.where(spot == place, 1.0, 0.0).astype(BF16)
    hi, lo = halves(basis_ref[...])
    pair = jnp.concatenate([hi, lo], 0)
    hot = hot_ref[...]
    turned_ref[...] = dot(hot, pair, ((1,), (1,))).astype(BF16)
    moved = dot(pair, hot, ((1,), (1,))).astype(BF16)
    whi, wlo = halves(w_ref[...])
    y = dot(moved, jnp.concatenate([whi, wlo], 1))
    y = y[0:rank, 0:width] + y[0:rank, width:] + y[rank:, 0:width]
    part_ref[...] = fine(first_ref[...], y, ((0,), (0,)))


def climb_kernel(flat_ref, part_ref, *refs):
    pairs, quads = refs[0:2], refs[2:6]
    keep_ref, send_ref, a_ref, b_ref = refs[6:]
    flat = flat_ref[0]
    half, quarter = pairs[0].shape[0], quads[0].shape[0]
    parity = flat % 2
    a_ref[...] = part_ref[...]
    total = None
    for k, ref in enumerate(pairs):
        at = pl.ds(pl.multiple_of((parity ^ k) * half, half), half)
        term = fine(ref[...], a_ref[at, :], ((0,), (0,)))
        total = term if total is None else total + term
    b_ref[...] = total
    total = None
    for k, ref in enumerate(quads):
        at = pl.ds(pl.multiple_of(((flat % 4) ^ k) * quarter, quarter), quarter)
        term = fine(ref[...], b_ref[at, :], ((0,), (0,)))
        total = term if total is None else total + term
    a_ref[...] = total
    keep_ref[...] = a_ref[pl.ds(pl.multiple_of(parity * half, half), half), :]
    send_ref[...] = a_ref[pl.ds(pl.multiple_of((1 - parity) * half, half), half), :]


def far_points_kernel(nodes, flat_ref, lists_ref, own_ref, mate_ref, out_ref, pts_ref):
    flat = flat_ref[0]
    rows = own_ref.shape[2]
    rank = rows * NODE
    node, position = flat // NODE, flat % NODE
    for k, ref in enumerate((own_ref, mate_ref)):
        for m in range(nodes):
            for r in range(NODE // 2):
                at = (node ^ m) * rank + (position ^ (2 * r) ^ k) * rows
                pts_ref[pl.ds(pl.multiple_of(at, rows), rows), :] = ref[m, r].astype(F32)
    feats = pts_ref.shape[1]
    left = pts_ref[pl.ds(pl.multiple_of(node * rank, rank), rank), :].astype(BF16)
    length, inv = norms(left)
    for m in range(nodes):
        at = pl.ds(m * rank, rank)
        pts = pts_ref[at, :]
        row = fine(jnp.ones((8, feats), F32), pts * pts, ((1,), (1,)))
        square = jnp.maximum(row[0:1, :], TINY)
        back = lax.rsqrt(square)
        c = dot(left, pts.astype(BF16), ((1,), (1,)))
        scale = jnp.where(listed(lists_ref, node, m), 0.5, 0.0)
        out_ref[:, m * rank : (m + 1) * rank] = unit_kernel(c * inv * back) * (
            length * (square * back * scale)
        )


def far_kernel(nodes, flat_ref, kern_ref, v_ref, vm_ref, b1_ref, *refs):
    pairs, quads = refs[0:2], refs[2:6]
    turned_ref, out_ref, w_ref, a_ref, b_ref = refs[6:]
    flat = flat_ref[0]
    rank = b1_ref.shape[1]
    half, quarter = pairs[0].shape[0], quads[0].shape[0]
    node, parity = flat // NODE, flat % 2
    for m in range(nodes):
        for k, ref in enumerate((v_ref, vm_ref)):
            at = (node ^ m) * rank + (parity ^ k) * half
            w_ref[pl.ds(pl.multiple_of(at, half), half), :] = ref[m]
    up = fine(kern_ref[...], w_ref[...])
    for k, ref in enumerate(quads):
        at = pl.ds(pl.multiple_of(((flat % 4) ^ k) * quarter, quarter), quarter)
        a_ref[at, :] = fine(ref[...], up)
    up = a_ref[...]
    for k, ref in enumerate(pairs):
        at = pl.ds(pl.multiple_of((parity ^ k) * half, half), half)
        b_ref[at, :] = fine(ref[...], up)
    up = fine(b1_ref[...], b_ref[...])
    hi, lo = halves(up)
    top = jnp.concatenate([hi, lo], 1)
    low = jnp.concatenate([hi, jnp.zeros_like(lo)], 1)
    far = dot(turned_ref[...], jnp.concatenate([top, low], 0))
    width = out_ref.shape[1]
    out_ref[...] = far[:, 0:width] + far[:, width:]


def join_kernel(a_ref, b_ref, c_ref, out_ref):
    out_ref[...] = a_ref[...] + b_ref[...] + c_ref[...]


def body(
    points, rhs, permutation, leaf_basis, climb_leaf, climb_pair, climb_quad, skel_points,
    near_lists, far_lists
):
    size, feats = points.shape
    width = rhs.shape[1]
    rank = climb_leaf.shape[1]
    nodes = lax.axis_size(AXES) // NODE
    flat = lax.axis_index(AXES).astype(jnp.int32).reshape(1)
    struct = jax.ShapeDtypeStruct

    quads = [climb_quad] + [across(climb_quad, k) for k in (1, 2, 3)]
    pairs = [climb_pair, across(climb_pair, 1)]
    four = jnp.stack([skel_points] + [across(skel_points, k) for k in (2, 4, 6)])

    mate_pts = across(points, 1)
    pack_shape = struct((size // 2 + 32, max(feats + 2 * width, size // 2)), BF16)
    pack_a, pack_b = call(pack_kernel, [pack_shape, pack_shape], 0, (points, rhs))
    x_a, y_a = across(pack_a, 2), across(pack_a, 4)
    x_b, y_b = across(pack_b, 2), across(pack_b, 4)
    d_a = across(y_a, 2)
    d_b = across(x_b, 4)
    masks = [NODE * m for m in range(1, nodes)]
    own_skel = jnp.stack([four] + [across(four, m) for m in masks])
    mate_skel = across(own_skel, 1)

    block = 2 * size * size * (feats + 6 * width) * 4
    sums = struct((size, width), F32)

    def near(masks, packs, before, last=False):
        kernel = functools.partial(near_kernel, masks, before is None, last)
        before = () if before is None else (before,)
        return call(
            kernel, [sums, sums] if last else struct((2, size, width), F32), 2,
            (flat, near_lists, points, mate_pts, *packs, *before),
            [
                pltpu.VMEM((2, size, feats), BF16),
                pltpu.VMEM((len(masks), *pack_shape.shape), BF16),
                pltpu.VMEM((2, size, 1), F32),
                pltpu.VMEM((2, size, width), F32),
                pltpu.SMEM((2 * len(masks),), jnp.int32),
            ],
            flops=block * len(masks) // 2,
        )

    turned, part = call(
        basis_kernel,
        [struct((size, 2 * rank), BF16), struct((rank, width), F32)],
        0,
        (permutation.reshape(1, size), leaf_basis, rhs, climb_leaf),
        [pltpu.VMEM((size, size), BF16)],
        flops=2 * size * size * rank * 6,
    )
    strip = struct((rank // 2, width), F32)
    keep, send = call(
        climb_kernel, [strip, strip], 1, (flat, part, *pairs, *quads),
        [pltpu.VMEM((rank, width), F32), pltpu.VMEM((rank, width), F32)],
        flops=2 * rank * rank * width * 12,
    )
    value = keep + across(send, 1)
    value = (value + across(value, 2)) + (across(value, 4) + across(value, 6))
    every = jnp.stack([value] + [across(value, m) for m in masks])
    every_mate = across(every, 1)

    kern = call(
        functools.partial(far_points_kernel, nodes),
        struct((rank, nodes * rank), F32),
        2,
        (flat, far_lists, own_skel, mate_skel),
        [pltpu.VMEM((nodes * rank, feats), F32)],
        flops=2 * rank * rank * feats * nodes * 4,
    )

    total = near((0, 0), (pack_a, pack_b), None)
    total = near((2, 4), (x_a, y_a), total)
    total = near((2, 4), (x_b, y_b), total)
    far = call(
        functools.partial(far_kernel, nodes),
        sums,
        1,
        (flat, kern, every, every_mate, climb_leaf, *pairs, *quads, turned),
        [
            pltpu.VMEM((nodes * rank, width), F32),
            pltpu.VMEM((rank, width), F32),
            pltpu.VMEM((rank, width), F32),
        ],
        flops=2 * rank * rank * width * 60,
    )
    mine, other = near((6, 6), (d_a, d_b), total, True)
    return call(join_kernel, sums, 0, (mine, across(other, 1), far))


def solution(mesh):
    split = P(AXES, None)

    return jax.shard_map(
        body,
        mesh=mesh,
        in_specs=(split, split, P(AXES), split, split, split, split, split, P(), P()),
        out_specs=split,
        check_vma=False,
    )
```

profile of v0, /device:TPU:7, one launch (start us, length us, event | category | flops | bytes accessed | tf_op | source)
XLA Modules:
  0.0 86.8 jit_solution(14511116287770470138)
XLA Ops:
  0.0 0.7 collective-permute-start.16
  0.7 0.3 collective-permute-start.17
  0.9 1.4 %collective-permute-start.18 = (f32[64,256]{1,0:T(8,128)}, f32[64,256]{1,0:T(8,128)S(1)}, u32[]{:S(2)}, u32[]{:S(2)}) collective-permute-start(f32[64,256]{1,0:T(8,128)} %refs_2_.11), channel_id=1, source_target_pairs={{0,3},{1,2},{2,1},{3,0},{4,7},{5,6},{6,5},{7,4},{8,11},{9,10},{10,... | collective-permute-start | bytes 196616 | tf_op jit(solution)/shard_map/ppermute | solution.py:32
  2.3 0.2 collective-permute-start.15
  2.5 0.3 collective-permute-start
  2.8 1.0 %copy-done = f32[1024,128]{1,0:T(8,128)S(1)} copy-done((f32[1024,128]{1,0:T(8,128)S(1)}, f32[1024,128]{1,0:T(8,128)}, u32[]{:S(2)}) %copy-start) | copy-done | bytes 524312
  3.9 0.9 %copy-done.3 = f32[256,256]{1,0:T(8,128)S(1)} copy-done((f32[256,256]{1,0:T(8,128)S(1)}, f32[256,256]{1,0:T(8,128)}, u32[]{:S(2)}) %copy-start.3) | copy-done | bytes 262168
  4.8 1.2 %copy-done.7 = f32[256,1024]{1,0:T(8,128)S(1)} copy-done((f32[256,1024]{1,0:T(8,128)S(1)}, f32[256,1024]{1,0:T(8,128)}, u32[]{:S(2)}) %copy-start.7) | copy-done | bytes 1048600
  6.0 0.7 copy-done.10
  6.7 3.4 %shard_map.106 = (bf16[1024,512]{1,0:T(8,128)(2,1)S(1)}, f32[256,128]{1,0:T(8,128)S(1)}) custom-call(s32[1,1024]{1,0:T(1,128)S(1)} %bitcast.15, f32[256,1024]{1,0:T(8,128)S(1)} %copy-done.7, f32[1024,128]{1,0:T(8,128)S(1)} %copy-done, f32[256,256]{1,0:T(8,128)S(1)} %copy-done.3), custom_call_target="tpu_custom_call" | custom-call | flops 3221225472 | tf_op jit(solution)/shard_map/pallas_call | solution.py:39
  10.1 0.0 copy-start.1
  10.1 0.0 collective-permute-done.16.refs_3_
  10.2 0.0 collective-permute-done.15.refs_1_
  10.2 0.0 copy-start.12
  10.2 1.4 %shard_map.107 = (f32[128,128]{1,0:T(8,128)S(1)}, f32[128,128]{1,0:T(8,128)S(1)}) custom-call(s32[1]{0:T(128)} %bitcast.refs_0_.flat_ref, f32[256,128]{1,0:T(8,128)S(1)} %get-tuple-element.17.part_ref, f32[128,256]{1,0:T(8,128)S(1)} %copy-done.5, f32[128,256]{1,0:T(8,128)S(1)} %collective-permute-done.15.refs_1_, f32[64,256]{1,0:T(8,128)S(1)} %copy-done.6, ...), custom_call_target="tpu_custom_call" | custom-call | flops 201326592 | tf_op jit(solution)/shard_map/pallas_call | solution.py:39
  11.6 0.3 collective-permute-start.19
  11.9 0.2 collective-permute-start.8
  12.2 0.0 collective-permute-start.9
  12.2 2.4 %collective-permute-start.10 = (bf16[32,256]{1,0:T(8,128)(2,1)S(1)}, bf16[32,256]{1,0:T(8,128)(2,1)S(1)}, u32[]{:S(2)}, u32[]{:S(2)}) collective-permute-start(bf16[32,256]{1,0:T(8,128)(2,1)S(1)} %copy-done.12), channel_id=1, source_target_pairs={{0,6},{1,7},{2,4},{3,5},{4,2},{5,3},{6,0},{7,1},{8,14},{9,15},{10,... | collective-permute-start | bytes 49160 | tf_op jit(solution)/shard_map/ppermute | solution.py:32
  14.6 1.0 %shard_map.100 = (bf16[544,512]{1,0:T(8,128)(2,1)S(1)}, bf16[544,512]{1,0:T(8,128)(2,1)S(1)}) custom-call(bf16[1024,256]{1,0:T(8,128)(2,1)S(1)} %copy-done.2, f32[1024,128]{1,0:T(8,128)S(1)} %copy-done.1), custom_call_target="tpu_custom_call" | custom-call | tf_op jit(solution)/shard_map/pallas_call | solution.py:39
  15.6 0.8 copy-done.8
  16.4 0.1 copy.14.refs_1_
  16.4 0.0 collective-permute-done.19
  16.4 0.3 collective-permute-start.1
  16.7 0.1 collective-permute-start.20
  16.9 0.0 collective-permute-done.9
  16.9 1.4 %collective-permute-start.21 = (f32[128,128]{1,0:T(8,128)S(1)}, f32[128,128]{1,0:T(8,128)S(1)}, u32[]{:S(2)}, u32[]{:S(2)}) collective-permute-start(f32[128,128]{1,0:T(8,128)S(1)} %add.16), channel_id=1, source_target_pairs={{0,4},{1,5},{2,6},{3,7},{4,0},{5,1},{6,2},{7,3},{8,12},{9,13},{10,... | collective-permute-start | bytes 196616 | tf_op jit(solution)/shard_map/ppermute | solution.py:32
  18.3 0.0 collective-permute-done.10
  18.3 1.2 %collective-permute-start.22 = (f32[128,128]{1,0:T(8,128)S(1)}, f32[128,128]{1,0:T(8,128)S(1)}, u32[]{:S(2)}, u32[]{:S(2)}) collective-permute-start(f32[128,128]{1,0:T(8,128)S(1)} %add.16), channel_id=1, source_target_pairs={{0,6},{1,7},{2,4},{3,5},{4,2},{5,3},{6,0},{7,1},{8,14},{9,15},{10,... | collective-permute-start | bytes 196616 | tf_op jit(solution)/shard_map/ppermute | solution.py:32
  19.5 0.4 collective-permute-done.20
  19.9 0.1 collective-permute-start.6
  20.0 12.6 %collective-permute-done.21 = f32[128,128]{1,0:T(8,128)S(1)} collective-permute-done((f32[128,128]{1,0:T(8,128)S(1)}, f32[128,128]{1,0:T(8,128)S(1)}, u32[]{:S(2)}, u32[]{:S(2)}) %collective-permute-start.21) | collective-permute-done | bytes 65568 | tf_op jit(solution)/shard_map/ppermute | solution.py:32
  32.6 0.2 collective-permute-start.3
  32.8 0.0 collective-permute-done.22
  32.8 0.6 collective-permute-start.5
  33.5 1.0 %collective-permute-start.11 = (bf16[4,32,256]{2,1,0:T(8,128)(2,1)S(1)}, bf16[4,32,256]{2,1,0:T(8,128)(2,1)S(1)}, u32[]{:S(2)}, u32[]{:S(2)}) collective-permute-start(bf16[4,32,256]{2,1,0:T(8,128)(2,1)S(1)} %get-tuple-element.22), channel_id=1, source_target_pairs={{0,8},{1,9},{2,10},{3,11},{4,12},{5,13},{6,14},{7,15},{8,0},{9,1},... | collective-permute-start | bytes 196616 | tf_op jit(solution)/shard_map/ppermute | solution.py:32
  34.5 6.1 %shard_map.101.refs_6_ = f32[2,1024,128]{2,1,0:T(8,128)S(1)} custom-call(s32[1]{0:T(128)} %bitcast.refs_0_.flat_ref, s32[32,8]{1,0:T(8,128)S(1)} %copy.14.refs_1_, bf16[1024,256]{1,0:T(8,128)(2,1)S(1)} %copy-done.2, bf16[1024,256]{1,0:T(8,128)(2,1)} %collective-permute-done.refs_3_, bf16[544,512]{1,0:T(8,128)(2,1)S(1)} %copy-done.9, ...), custom_call_target="tpu_custom_call" | custom-call | flops 8589934592 | tf_op jit(solution)/shard_map/pallas_call | solution.py:39
  40.7 0.0 collective-permute-done.1.refs_5_
  40.7 2.4 %collective-permute-start.12 = (bf16[4,32,256]{2,1,0:T(8,128)(2,1)S(1)}, bf16[4,32,256]{2,1,0:T(8,128)(2,1)S(1)}, u32[]{:S(2)}, u32[]{:S(2)}) collective-permute-start(bf16[4,32,256]{2,1,0:T(8,128)(2,1)S(1)} %get-tuple-element.22), channel_id=1, source_target_pairs={{0,16},{1,17},{2,18},{3,19},{4,20},{5,21},{6,22},{7,23},{8,24},{9,... | collective-permute-start | bytes 196616 | tf_op jit(solution)/shard_map/ppermute | solution.py:32
  43.0 0.3 collective-permute-start.13
  43.3 1.4 %shard_map.102.refs_6_ = f32[2,1024,128]{2,1,0:T(8,128)S(1)} custom-call(s32[1]{0:T(128)} %bitcast.refs_0_.flat_ref, s32[32,8]{1,0:T(8,128)S(1)} %copy.14.refs_1_, bf16[1024,256]{1,0:T(8,128)(2,1)S(1)} %copy-done.2, bf16[1024,256]{1,0:T(8,128)(2,1)} %collective-permute-done.refs_3_, bf16[544,512]{1,0:T(8,128)(2,1)S(1)} %collective-permute-done.6.refs_4_, ...), custom_call_target="tpu_custom_call" | custom-call | flops 8589934592 | tf_op jit(solution)/shard_map/pallas_call | solution.py:39
  44.8 0.4 collective-permute-done.3.refs_4_
  45.2 5.0 %collective-permute-start.2 = (bf16[544,512]{1,0:T(8,128)(2,1)S(1)}, bf16[544,512]{1,0:T(8,128)(2,1)S(1)}, u32[]{:S(2)}, u32[]{:S(2)}) collective-permute-start(bf16[544,512]{1,0:T(8,128)(2,1)S(1)} %collective-permute-done.1.refs_5_), channel_id=1, source_target_pairs={{0,2},{1,3},{2,0},{3,1},{4,6},{5,7},{6,4},{7,5},{8,10},{9,11},{10,... | collective-permute-start | bytes 1671176 | tf_op jit(solution)/shard_map/ppermute | solution.py:32
  50.2 1.2 %collective-permute-start.4 = (bf16[544,512]{1,0:T(8,128)(2,1)S(1)}, bf16[544,512]{1,0:T(8,128)(2,1)S(1)}, u32[]{:S(2)}, u32[]{:S(2)}) collective-permute-start(bf16[544,512]{1,0:T(8,128)(2,1)S(1)} %collective-permute-done.3.refs_4_), channel_id=1, source_target_pairs={{0,4},{1,5},{2,6},{3,7},{4,0},{5,1},{6,2},{7,3},{8,12},{9,13},{10,... | collective-permute-start | bytes 1671176 | tf_op jit(solution)/shard_map/ppermute | solution.py:32
  51.4 1.4 %shard_map.103.refs_6_ = f32[2,1024,128]{2,1,0:T(8,128)S(1)} custom-call(s32[1]{0:T(128)} %bitcast.refs_0_.flat_ref, s32[32,8]{1,0:T(8,128)S(1)} %copy.14.refs_1_, bf16[1024,256]{1,0:T(8,128)(2,1)S(1)} %copy-done.2, bf16[1024,256]{1,0:T(8,128)(2,1)} %collective-permute-done.refs_3_, bf16[544,512]{1,0:T(8,128)(2,1)S(1)} %collective-permute-done.3.refs_4_, ...), custom_call_target="tpu_custom_call" | custom-call | flops 8589934592 | tf_op jit(solution)/shard_map/pallas_call | solution.py:39
  52.9 9.2 %collective-permute-done.2.refs_4_ = bf16[544,512]{1,0:T(8,128)(2,1)S(1)} collective-permute-done((bf16[544,512]{1,0:T(8,128)(2,1)S(1)}, bf16[544,512]{1,0:T(8,128)(2,1)S(1)}, u32[]{:S(2)}, u32[]{:S(2)}) %collective-permute-start.2) | collective-permute-done | bytes 557088 | tf_op jit(solution)/shard_map/ppermute | solution.py:32
  62.0 0.4 collective-permute-start.23
  62.5 0.0 collective-permute-done.4.refs_5_
  62.5 2.6 %collective-permute-start.24 = (f32[128,128]{1,0:T(8,128)S(1)}, f32[128,128]{1,0:T(8,128)S(1)}, u32[]{:S(2)}, u32[]{:S(2)}) collective-permute-start(f32[128,128]{1,0:T(8,128)S(1)} %add_add_fusion), channel_id=1, source_target_pairs={{0,16},{1,17},{2,18},{3,19},{4,20},{5,21},{6,22},{7,23},{8,24},{9,... | collective-permute-start | bytes 196616 | tf_op jit(solution)/shard_map/ppermute | solution.py:32
  65.1 1.6 %shard_map.104 = (f32[1024,128]{1,0:T(8,128)S(1)}, f32[1024,128]{1,0:T(8,128)S(1)}) custom-call(s32[1]{0:T(128)} %bitcast.refs_0_.flat_ref, s32[32,8]{1,0:T(8,128)S(1)} %copy.14.refs_1_, bf16[1024,256]{1,0:T(8,128)(2,1)S(1)} %copy-done.2, bf16[1024,256]{1,0:T(8,128)(2,1)} %collective-permute-done.refs_3_, ...), custom_call_target="tpu_custom_call" | custom-call | flops 8589934592 | tf_op jit(solution)/shard_map/pallas_call | solution.py:39
  66.8 0.0 collective-permute-done.11
  66.8 0.9 %collective-permute-start.25 = (f32[128,128]{1,0:T(8,128)S(1)}, f32[128,128]{1,0:T(8,128)S(1)}, u32[]{:S(2)}, u32[]{:S(2)}) collective-permute-start(f32[128,128]{1,0:T(8,128)S(1)} %add_add_fusion), channel_id=1, source_target_pairs={{0,24},{1,25},{2,26},{3,27},{4,28},{5,29},{6,30},{7,31},{8,16},{9,... | collective-permute-start | bytes 196616 | tf_op jit(solution)/shard_map/ppermute | solution.py:32
  67.7 0.0 collective-permute-done.12
  67.7 5.6 %collective-permute-start.7 = (f32[1024,128]{1,0:T(8,128)S(1)}, f32[1024,128]{1,0:T(8,128)S(1)}, u32[]{:S(2)}, u32[]{:S(2)}) collective-permute-start(f32[1024,128]{1,0:T(8,128)S(1)} %get-tuple-element.16), channel_id=1, source_target_pairs={{0,1},{1,0},{2,3},{3,2},{4,5},{5,4},{6,7},{7,6},{8,9},{9,8},{10,11... | collective-permute-start | bytes 1572872 | tf_op jit(solution)/shard_map/ppermute | solution.py:32
  73.3 0.1 collective-permute-start.14
  73.4 0.0 collective-permute-done.23
  73.4 0.0 collective-permute-done.24
  73.4 0.0 collective-permute-done.25
  73.4 0.0 copy-start.11
  73.5 0.0 copy-start.4
  73.5 5.9 %collective-permute-start.26 = (f32[4,128,128]{2,1,0:T(8,128)S(1)}, f32[4,128,128]{2,1,0:T(8,128)S(1)}, u32[]{:S(2)}, u32[]{:S(2)}) collective-permute-start(f32[4,128,128]{2,1,0:T(8,128)S(1)} %pad_maximum_fusion.1.v_ref), channel_id=1, source_target_pairs={{0,1},{1,0},{2,3},{3,2},{4,5},{5,4},{6,7},{7,6},{8,9},{9,8},{10,11... | collective-permute-start | bytes 786440 | tf_op jit(solution)/shard_map/ppermute | solution.py:32
  79.4 2.5 %shard_map.105.kern_ref = f32[256,1024]{1,0:T(8,128)S(1)} custom-call(s32[1]{0:T(128)} %bitcast.refs_0_.flat_ref, s32[4,3]{1,0:T(4,128)S(1)} %copy-done.11, bf16[4,4,32,256]{3,2,1,0:T(8,128)(2,1)S(1)} %pad_maximum_fusion.own_ref, bf16[4,4,32,256]{3,2,1,0:T(8,128)(2,1)S(1)} %collective-permute-done.14.mate_ref), custom_call_target="tpu_custom_call" | custom-call | flops 536870912 | tf_op jit(solution)/shard_map/pallas_call | solution.py:39
  81.8 4.1 %shard_map.108.c_ref = f32[1024,128]{1,0:T(8,128)S(1)} custom-call(s32[1]{0:T(128)} %bitcast.refs_0_.flat_ref, f32[256,1024]{1,0:T(8,128)S(1)} %shard_map.105.kern_ref, f32[4,128,128]{2,1,0:T(8,128)S(1)} %pad_maximum_fusion.1.v_ref, f32[4,128,128]{2,1,0:T(8,128)S(1)} %collective-permute-done.26.vm_ref, f32[256,256]{1,0:T(8,128)S(1)} %copy-done.4, ...), custom_call_target="tpu_custom_call" | custom-call | flops 1006632960 | tf_op jit(solution)/shard_map/pallas_call | solution.py:39
  85.9 0.9 %shard_map.109 = f32[1024,128]{1,0:T(8,128)} custom-call(f32[1024,128]{1,0:T(8,128)S(1)} %get-tuple-element.15.a_ref, f32[1024,128]{1,0:T(8,128)S(1)} %collective-permute-done.7.b_ref, f32[1024,128]{1,0:T(8,128)S(1)} %shard_map.108.c_ref), custom_call_target="tpu_custom_call" | custom-call | tf_op jit(solution)/shard_map/pallas_call | solution.py:39
  (34 shorter events, 0.2 us)
Async XLA Ops:
  0.0 10.1 %collective-permute-start.16 = (f32[64,256]{1,0:T(8,128)}, f32[64,256]{1,0:T(8,128)S(1)}, u32[]{:S(2)}, u32[]{:S(2)}) collective-permute-start(f32[64,256]{1,0:T(8,128)} %refs_2_.11), channel_id=1, source_target_pairs={{0,1},{1,0},{2,3},{3,2},{4,5},{5,4},{6,7},{7,6},{8,9},{9,8},{10,11... | collective-permute-start | bytes 196616 | tf_op jit(solution)/shard_map/ppermute | solution.py:32
  0.7 9.5 %collective-permute-start.17 = (f32[64,256]{1,0:T(8,128)}, f32[64,256]{1,0:T(8,128)S(1)}, u32[]{:S(2)}, u32[]{:S(2)}) collective-permute-start(f32[64,256]{1,0:T(8,128)} %refs_2_.11), channel_id=1, source_target_pairs={{0,2},{1,3},{2,0},{3,1},{4,6},{5,7},{6,4},{7,5},{8,10},{9,11},{10,... | collective-permute-start | bytes 196616 | tf_op jit(solution)/shard_map/ppermute | solution.py:32
  0.9 9.2 %collective-permute-start.18 = (f32[64,256]{1,0:T(8,128)}, f32[64,256]{1,0:T(8,128)S(1)}, u32[]{:S(2)}, u32[]{:S(2)}) collective-permute-start(f32[64,256]{1,0:T(8,128)} %refs_2_.11), channel_id=1, source_target_pairs={{0,3},{1,2},{2,1},{3,0},{4,7},{5,6},{6,5},{7,4},{8,11},{9,10},{10,... | collective-permute-start | bytes 196616 | tf_op jit(solution)/shard_map/ppermute | solution.py:32
  2.3 7.9 %collective-permute-start.15 = (f32[128,256]{1,0:T(8,128)}, f32[128,256]{1,0:T(8,128)S(1)}, u32[]{:S(2)}, u32[]{:S(2)}) collective-permute-start(f32[128,256]{1,0:T(8,128)} %refs_0_.3), channel_id=1, source_target_pairs={{0,1},{1,0},{2,3},{3,2},{4,5},{5,4},{6,7},{7,6},{8,9},{9,8},{10,11... | collective-permute-start | bytes 393224 | tf_op jit(solution)/shard_map/ppermute | solution.py:32
  2.5 30.9 %collective-permute-start = (bf16[1024,256]{1,0:T(8,128)(2,1)}, bf16[1024,256]{1,0:T(8,128)(2,1)}, u32[]{:S(2)}, u32[]{:S(2)}) collective-permute-start(bf16[1024,256]{1,0:T(8,128)(2,1)} %refs_2_.9), channel_id=1, source_target_pairs={{0,1},{1,0},{2,3},{3,2},{4,5},{5,4},{6,7},{7,6},{8,9},{9,8},{10,11... | collective-permute-start | bytes 1572872 | tf_op jit(solution)/shard_map/ppermute | solution.py:32
  2.8 1.0 %copy-start = (f32[1024,128]{1,0:T(8,128)S(1)}, f32[1024,128]{1,0:T(8,128)}, u32[]{:S(2)}) copy-start(f32[1024,128]{1,0:T(8,128)} %w_ref.3) | copy-start | bytes 1572868
  3.9 0.9 %copy-start.3 = (f32[256,256]{1,0:T(8,128)S(1)}, f32[256,256]{1,0:T(8,128)}, u32[]{:S(2)}) copy-start(f32[256,256]{1,0:T(8,128)} %b1_ref.1) | copy-start | bytes 786436
  4.8 1.2 %copy-start.7 = (f32[256,1024]{1,0:T(8,128)S(1)}, f32[256,1024]{1,0:T(8,128)}, u32[]{:S(2)}) copy-start(f32[256,1024]{1,0:T(8,128)} %basis_ref.1) | copy-start | bytes 3145732
  6.0 0.7 copy-start.10
  6.7 3.5 %copy-start.5 = (f32[128,256]{1,0:T(8,128)S(1)}, f32[128,256]{1,0:T(8,128)}, u32[]{:S(2)}) copy-start(f32[128,256]{1,0:T(8,128)} %refs_0_.3) | copy-start | bytes 393220
  6.7 3.5 %copy-start.6 = (f32[64,256]{1,0:T(8,128)S(1)}, f32[64,256]{1,0:T(8,128)}, u32[]{:S(2)}) copy-start(f32[64,256]{1,0:T(8,128)} %refs_2_.11) | copy-start | bytes 196612
  6.7 7.8 %copy-start.2 = (bf16[1024,256]{1,0:T(8,128)(2,1)S(1)}, bf16[1024,256]{1,0:T(8,128)(2,1)}, u32[]{:S(2)}) copy-start(bf16[1024,256]{1,0:T(8,128)(2,1)} %refs_2_.9) | copy-start | bytes 1572868
  10.1 4.4 %copy-start.1 = (f32[1024,128]{1,0:T(8,128)S(1)}, f32[1024,128]{1,0:T(8,128)}, u32[]{:S(2)}) copy-start(f32[1024,128]{1,0:T(8,128)} %w_ref.3) | copy-start | bytes 1572868
  10.2 1.7 %copy-start.12 = (bf16[32,256]{1,0:T(8,128)(2,1)S(1)}, bf16[32,256]{1,0:T(8,128)(2,1)}, u32[]{:S(2)}) copy-start(bf16[32,256]{1,0:T(8,128)(2,1)} %param.17) | copy-start | bytes 49156
  11.6 4.8 %copy-start.13 = (s32[32,8]{0,1:T(8,128)S(1)}, s32[32,8]{0,1:T(8,128)}, u32[]{:S(2)}) copy-start(s32[32,8]{0,1:T(8,128)} %param.18) | copy-start | bytes 3076
  11.6 4.8 %collective-permute-start.19 = (f32[128,128]{1,0:T(8,128)S(1)}, f32[128,128]{1,0:T(8,128)S(1)}, u32[]{:S(2)}, u32[]{:S(2)}) collective-permute-start(f32[128,128]{1,0:T(8,128)S(1)} %get-tuple-element.19), channel_id=1, source_target_pairs={{0,1},{1,0},{2,3},{3,2},{4,5},{5,4},{6,7},{7,6},{8,9},{9,8},{10,11... | collective-permute-start | bytes 196616 | tf_op jit(solution)/shard_map/ppermute | solution.py:32
  11.9 4.8 %collective-permute-start.8 = (bf16[32,256]{1,0:T(8,128)(2,1)S(1)}, bf16[32,256]{1,0:T(8,128)(2,1)S(1)}, u32[]{:S(2)}, u32[]{:S(2)}) collective-permute-start(bf16[32,256]{1,0:T(8,128)(2,1)S(1)} %copy-done.12), channel_id=1, source_target_pairs={{0,2},{1,3},{2,0},{3,1},{4,6},{5,7},{6,4},{7,5},{8,10},{9,11},{10,... | collective-permute-start | bytes 49160 | tf_op jit(solution)/shard_map/ppermute | solution.py:32
  12.2 4.7 %collective-permute-start.9 = (bf16[32,256]{1,0:T(8,128)(2,1)S(1)}, bf16[32,256]{1,0:T(8,128)(2,1)S(1)}, u32[]{:S(2)}, u32[]{:S(2)}) collective-permute-start(bf16[32,256]{1,0:T(8,128)(2,1)S(1)} %copy-done.12), channel_id=1, source_target_pairs={{0,4},{1,5},{2,6},{3,7},{4,0},{5,1},{6,2},{7,3},{8,12},{9,13},{10,... | collective-permute-start | bytes 49160 | tf_op jit(solution)/shard_map/ppermute | solution.py:32
  12.2 6.1 %collective-permute-start.10 = (bf16[32,256]{1,0:T(8,128)(2,1)S(1)}, bf16[32,256]{1,0:T(8,128)(2,1)S(1)}, u32[]{:S(2)}, u32[]{:S(2)}) collective-permute-start(bf16[32,256]{1,0:T(8,128)(2,1)S(1)} %copy-done.12), channel_id=1, source_target_pairs={{0,6},{1,7},{2,4},{3,5},{4,2},{5,3},{6,0},{7,1},{8,14},{9,15},{10,... | collective-permute-start | bytes 49160 | tf_op jit(solution)/shard_map/ppermute | solution.py:32
  15.5 0.8 copy-start.8
  16.4 18.1 %copy-start.9 = (bf16[544,512]{1,0:T(8,128)(2,1)S(1)}, bf16[544,512]{1,0:T(8,128)(2,1)}, u32[]{:S(2)}) copy-start(bf16[544,512]{1,0:T(8,128)(2,1)} %copy-done.8) | copy-start | bytes 1671172
  16.4 24.2 %collective-permute-start.1 = (bf16[544,512]{1,0:T(8,128)(2,1)}, bf16[544,512]{1,0:T(8,128)(2,1)S(1)}, u32[]{:S(2)}, u32[]{:S(2)}) collective-permute-start(bf16[544,512]{1,0:T(8,128)(2,1)} %copy-done.8), channel_id=1, source_target_pairs={{0,4},{1,5},{2,6},{3,7},{4,0},{5,1},{6,2},{7,3},{8,12},{9,13},{10,... | collective-permute-start | bytes 1671176 | tf_op jit(solution)/shard_map/ppermute | solution.py:32
  16.7 3.2 %collective-permute-start.20 = (f32[128,128]{1,0:T(8,128)S(1)}, f32[128,128]{1,0:T(8,128)S(1)}, u32[]{:S(2)}, u32[]{:S(2)}) collective-permute-start(f32[128,128]{1,0:T(8,128)S(1)} %add.16), channel_id=1, source_target_pairs={{0,2},{1,3},{2,0},{3,1},{4,6},{5,7},{6,4},{7,5},{8,10},{9,11},{10,... | collective-permute-start | bytes 196616 | tf_op jit(solution)/shard_map/ppermute | solution.py:32
  16.9 15.7 %collective-permute-start.21 = (f32[128,128]{1,0:T(8,128)S(1)}, f32[128,128]{1,0:T(8,128)S(1)}, u32[]{:S(2)}, u32[]{:S(2)}) collective-permute-start(f32[128,128]{1,0:T(8,128)S(1)} %add.16), channel_id=1, source_target_pairs={{0,4},{1,5},{2,6},{3,7},{4,0},{5,1},{6,2},{7,3},{8,12},{9,13},{10,... | collective-permute-start | bytes 196616 | tf_op jit(solution)/shard_map/ppermute | solution.py:32
  18.3 14.5 %collective-permute-start.22 = (f32[128,128]{1,0:T(8,128)S(1)}, f32[128,128]{1,0:T(8,128)S(1)}, u32[]{:S(2)}, u32[]{:S(2)}) collective-permute-start(f32[128,128]{1,0:T(8,128)S(1)} %add.16), channel_id=1, source_target_pairs={{0,6},{1,7},{2,4},{3,5},{4,2},{5,3},{6,0},{7,1},{8,14},{9,15},{10,... | collective-permute-start | bytes 196616 | tf_op jit(solution)/shard_map/ppermute | solution.py:32
  19.9 23.1 %collective-permute-start.6 = (bf16[544,512]{1,0:T(8,128)(2,1)}, bf16[544,512]{1,0:T(8,128)(2,1)S(1)}, u32[]{:S(2)}, u32[]{:S(2)}) collective-permute-start(bf16[544,512]{1,0:T(8,128)(2,1)} %copy-done.8), channel_id=1, source_target_pairs={{0,2},{1,3},{2,0},{3,1},{4,6},{5,7},{6,4},{7,5},{8,10},{9,11},{10,... | collective-permute-start | bytes 1671176 | tf_op jit(solution)/shard_map/ppermute | solution.py:32
  32.6 12.6 %collective-permute-start.3 = (bf16[544,512]{1,0:T(8,128)(2,1)S(1)}, bf16[544,512]{1,0:T(8,128)(2,1)S(1)}, u32[]{:S(2)}, u32[]{:S(2)}) collective-permute-start(bf16[544,512]{1,0:T(8,128)(2,1)S(1)} %get-tuple-element.14.refs_5_), channel_id=1, source_target_pairs={{0,2},{1,3},{2,0},{3,1},{4,6},{5,7},{6,4},{7,5},{8,10},{9,11},{10,... | collective-permute-start | bytes 1671176 | tf_op jit(solution)/shard_map/ppermute | solution.py:32
  32.8 17.4 %collective-permute-start.5 = (bf16[544,512]{1,0:T(8,128)(2,1)S(1)}, bf16[544,512]{1,0:T(8,128)(2,1)S(1)}, u32[]{:S(2)}, u32[]{:S(2)}) collective-permute-start(bf16[544,512]{1,0:T(8,128)(2,1)S(1)} %get-tuple-element.14.refs_5_), channel_id=1, source_target_pairs={{0,4},{1,5},{2,6},{3,7},{4,0},{5,1},{6,2},{7,3},{8,12},{9,13},{10,... | collective-permute-start | bytes 1671176 | tf_op jit(solution)/shard_map/ppermute | solution.py:32
  33.5 33.3 %collective-permute-start.11 = (bf16[4,32,256]{2,1,0:T(8,128)(2,1)S(1)}, bf16[4,32,256]{2,1,0:T(8,128)(2,1)S(1)}, u32[]{:S(2)}, u32[]{:S(2)}) collective-permute-start(bf16[4,32,256]{2,1,0:T(8,128)(2,1)S(1)} %get-tuple-element.22), channel_id=1, source_target_pairs={{0,8},{1,9},{2,10},{3,11},{4,12},{5,13},{6,14},{7,15},{8,0},{9,1},... | collective-permute-start | bytes 196616 | tf_op jit(solution)/shard_map/ppermute | solution.py:32
  40.7 27.0 %collective-permute-start.12 = (bf16[4,32,256]{2,1,0:T(8,128)(2,1)S(1)}, bf16[4,32,256]{2,1,0:T(8,128)(2,1)S(1)}, u32[]{:S(2)}, u32[]{:S(2)}) collective-permute-start(bf16[4,32,256]{2,1,0:T(8,128)(2,1)S(1)} %get-tuple-element.22), channel_id=1, source_target_pairs={{0,16},{1,17},{2,18},{3,19},{4,20},{5,21},{6,22},{7,23},{8,24},{9,... | collective-permute-start | bytes 196616 | tf_op jit(solution)/shard_map/ppermute | solution.py:32
  43.0 30.2 %collective-permute-start.13 = (bf16[4,32,256]{2,1,0:T(8,128)(2,1)S(1)}, bf16[4,32,256]{2,1,0:T(8,128)(2,1)S(1)}, u32[]{:S(2)}, u32[]{:S(2)}) collective-permute-start(bf16[4,32,256]{2,1,0:T(8,128)(2,1)S(1)} %get-tuple-element.22), channel_id=1, source_target_pairs={{0,24},{1,25},{2,26},{3,27},{4,28},{5,29},{6,30},{7,31},{8,16},{9,... | collective-permute-start | bytes 196616 | tf_op jit(solution)/shard_map/ppermute | solution.py:32
  45.2 16.9 %collective-permute-start.2 = (bf16[544,512]{1,0:T(8,128)(2,1)S(1)}, bf16[544,512]{1,0:T(8,128)(2,1)S(1)}, u32[]{:S(2)}, u32[]{:S(2)}) collective-permute-start(bf16[544,512]{1,0:T(8,128)(2,1)S(1)} %collective-permute-done.1.refs_5_), channel_id=1, source_target_pairs={{0,2},{1,3},{2,0},{3,1},{4,6},{5,7},{6,4},{7,5},{8,10},{9,11},{10,... | collective-permute-start | bytes 1671176 | tf_op jit(solution)/shard_map/ppermute | solution.py:32
  50.2 12.3 %collective-permute-start.4 = (bf16[544,512]{1,0:T(8,128)(2,1)S(1)}, bf16[544,512]{1,0:T(8,128)(2,1)S(1)}, u32[]{:S(2)}, u32[]{:S(2)}) collective-permute-start(bf16[544,512]{1,0:T(8,128)(2,1)S(1)} %collective-permute-done.3.refs_4_), channel_id=1, source_target_pairs={{0,4},{1,5},{2,6},{3,7},{4,0},{5,1},{6,2},{7,3},{8,12},{9,13},{10,... | collective-permute-start | bytes 1671176 | tf_op jit(solution)/shard_map/ppermute | solution.py:32
  62.0 11.4 %collective-permute-start.23 = (f32[128,128]{1,0:T(8,128)S(1)}, f32[128,128]{1,0:T(8,128)S(1)}, u32[]{:S(2)}, u32[]{:S(2)}) collective-permute-start(f32[128,128]{1,0:T(8,128)S(1)} %add_add_fusion), channel_id=1, source_target_pairs={{0,8},{1,9},{2,10},{3,11},{4,12},{5,13},{6,14},{7,15},{8,0},{9,1},... | collective-permute-start | bytes 196616 | tf_op jit(solution)/shard_map/ppermute | solution.py:32
  62.5 10.9 %collective-permute-start.24 = (f32[128,128]{1,0:T(8,128)S(1)}, f32[128,128]{1,0:T(8,128)S(1)}, u32[]{:S(2)}, u32[]{:S(2)}) collective-permute-start(f32[128,128]{1,0:T(8,128)S(1)} %add_add_fusion), channel_id=1, source_target_pairs={{0,16},{1,17},{2,18},{3,19},{4,20},{5,21},{6,22},{7,23},{8,24},{9,... | collective-permute-start | bytes 196616 | tf_op jit(solution)/shard_map/ppermute | solution.py:32
  66.8 6.6 %collective-permute-start.25 = (f32[128,128]{1,0:T(8,128)S(1)}, f32[128,128]{1,0:T(8,128)S(1)}, u32[]{:S(2)}, u32[]{:S(2)}) collective-permute-start(f32[128,128]{1,0:T(8,128)S(1)} %add_add_fusion), channel_id=1, source_target_pairs={{0,24},{1,25},{2,26},{3,27},{4,28},{5,29},{6,30},{7,31},{8,16},{9,... | collective-permute-start | bytes 196616 | tf_op jit(solution)/shard_map/ppermute | solution.py:32
  67.7 18.2 %collective-permute-start.7 = (f32[1024,128]{1,0:T(8,128)S(1)}, f32[1024,128]{1,0:T(8,128)S(1)}, u32[]{:S(2)}, u32[]{:S(2)}) collective-permute-start(f32[1024,128]{1,0:T(8,128)S(1)} %get-tuple-element.16), channel_id=1, source_target_pairs={{0,1},{1,0},{2,3},{3,2},{4,5},{5,4},{6,7},{7,6},{8,9},{9,8},{10,11... | collective-permute-start | bytes 1572872 | tf_op jit(solution)/shard_map/ppermute | solution.py:32
  73.3 6.0 %collective-permute-start.14 = (bf16[4,4,32,256]{3,2,1,0:T(8,128)(2,1)S(1)}, bf16[4,4,32,256]{3,2,1,0:T(8,128)(2,1)S(1)}, u32[]{:S(2)}, u32[]{:S(2)}) collective-permute-start(bf16[4,4,32,256]{3,2,1,0:T(8,128)(2,1)S(1)} %pad_maximum_fusion.own_ref), channel_id=1, source_target_pairs={{0,1},{1,0},{2,3},{3,2},{4,5},{5,4},{6,7},{7,6},{8,9},{9,8},{10,11... | collective-permute-start | bytes 786440 | tf_op jit(solution)/shard_map/ppermute | solution.py:32
  73.4 5.9 %copy-start.11 = (s32[4,3]{1,0:T(4,128)S(1)}, s32[4,3]{1,0:T(4,128)}, u32[]{:S(2)}) copy-start(s32[4,3]{1,0:T(4,128)} %lists_ref.1) | copy-start | bytes 148
  73.5 8.4 %copy-start.4 = (f32[256,256]{1,0:T(8,128)S(1)}, f32[256,256]{1,0:T(8,128)}, u32[]{:S(2)}) copy-start(f32[256,256]{1,0:T(8,128)} %b1_ref.1) | copy-start | bytes 786436
  73.5 8.3 %collective-permute-start.26 = (f32[4,128,128]{2,1,0:T(8,128)S(1)}, f32[4,128,128]{2,1,0:T(8,128)S(1)}, u32[]{:S(2)}, u32[]{:S(2)}) collective-permute-start(f32[4,128,128]{2,1,0:T(8,128)S(1)} %pad_maximum_fusion.1.v_ref), channel_id=1, source_target_pairs={{0,1},{1,0},{2,3},{3,2},{4,5},{5,4},{6,7},{7,6},{8,9},{9,8},{10,11... | collective-permute-start | bytes 786440 | tf_op jit(solution)/shard_map/ppermute | solution.py:32
where the time goes:
time: 87.2 us; the launch traced here: 86.8 us
  starting transfers between devices  35.2 us (40%)
  Pallas kernels  23.7 us (27%)
  waiting for transfers between devices  22.7 us (26%)
  local copies, waits for them, and re-layouts  4.82 us (6%)
    ppermute x27, starting transfers between devices, across(): return lax.ppermute(value, AXES, pairs)  35.2 us
    pallas_call x10, Pallas kernels, call(): pl.pallas_call(kernel, out_shape=out, in_specs=specs, out_specs=[pl.Block...  23.7 us
    ppermute x27, waiting for transfers between devices, across(): return lax.ppermute(value, AXES, pairs)  22.7 us
    unnamed x29, local copies, waits for them, and re-layouts  4.82 us
  transfers between devices with their start and end apart: 27, of which 4 were waited for; matrix products, arithmetic and copies ran while one was open for 0% of the time, Pallas kernels for 26%

commit v1 on v0

v1 whole, which is shorter than its diff:
```python
import functools

import jax
import jax.numpy as jnp
from jax import lax
from jax.experimental import pallas as pl
from jax.experimental.pallas import tpu as pltpu
from jax.sharding import PartitionSpec as P


AXES = ("leaf", "grp")
NODE = 8
TINY = 1e-30
SERIES = (
    1.0000005285886142,
    -5.669123056911696e-05,
    -0.4990002868296516,
    0.20543817481505877,
    -0.10204939882030772,
    0.040449241962581796,
    -0.008162324706047165,
)
F32 = jnp.float32
BF16 = jnp.bfloat16
VMEM = pltpu.VMEM
SMEM = pltpu.SMEM


def across(value, mask):
    pairs = [(s, s ^ mask) for s in range(lax.axis_size(AXES))]
    return lax.ppermute(value, AXES, pairs)


def call(kernel, out, n_smem, operands, scratch=(), flops=0, loose=0,
         far_memory=False):
    specs = [pl.BlockSpec(memory_space=SMEM)] * n_smem
    specs += [pl.BlockSpec(memory_space=pltpu.MemorySpace.HBM if far_memory else pl.ANY)] * loose
    specs += [pl.BlockSpec(memory_space=VMEM)] * (len(operands) - n_smem - loose)
    multi = isinstance(out, (list, tuple))
    return pl.pallas_call(
        kernel,
        out_shape=out,
        in_specs=specs,
        out_specs=[pl.BlockSpec(memory_space=VMEM)] * len(out)
        if multi
        else pl.BlockSpec(memory_space=VMEM),
        scratch_shapes=list(scratch),
        cost_estimate=pl.CostEstimate(flops=flops, bytes_accessed=0, transcendentals=0),
        compiler_params=pltpu.CompilerParams(vmem_limit_bytes=40 * 2**20),
    )(*operands)


def halves(value):
    hi = value.astype(BF16)
    return hi, (value - hi.astype(F32)).astype(BF16)


def dot(a, b, dims=((1,), (0,))):
    return lax.dot_general(a, b, (dims, ((), ())), preferred_element_type=F32)


def three(a, b, dims=((1,), (0,))):
    ahi, alo = halves(a)
    wide = jnp.concatenate(halves(b), 1)
    width = b.shape[1]
    total = dot(ahi, wide, dims) + dot(alo, wide, dims)
    return total[:, 0:width] + total[:, width:]


def unit_kernel(cosine):
    z = jnp.maximum(1.0 - cosine * cosine, TINY)
    w = z * lax.rsqrt(z)
    acc = jnp.full_like(w, SERIES[-1])
    for coef in SERIES[-2::-1]:
        acc = acc * w + coef
    return acc + cosine


def norms(x):
    x = x.astype(F32)
    sq = jnp.maximum(jnp.sum(x * x, axis=1, keepdims=True), TINY)
    inv = lax.rsqrt(sq)
    return sq * inv, inv


def pack_kernel(x_hbm, w_hbm, a_ref, b_ref, x_ref, w_ref, sem):
    half = x_ref.shape[0] // 2
    width = w_ref.shape[1]
    feats = x_ref.shape[1]
    moves = []
    for k in range(2):
        rows = pl.ds(k * half, half)
        for j, (src, dst) in enumerate(((x_hbm, x_ref), (w_hbm, w_ref))):
            move = pltpu.make_async_copy(src.at[rows, :], dst.at[rows, :], sem.at[2 * k + j])
            move.start()
            moves.append(move)
    for k, ref in enumerate((a_ref, b_ref)):
        rows = pl.ds(k * half, half)
        moves[2 * k].wait()
        moves[2 * k + 1].wait()
        x = x_ref[rows, :]
        ref[0:half, 0:feats] = x
        xf = x.astype(F32)
        length, _ = norms(x)
        hi, lo = halves(w_ref[rows, :] * (length * 0.5))
        ref[0:half, feats : feats + width] = hi
        ref[0:half, feats + width : feats + 2 * width] = lo
        shi, slo = halves(xf * xf)
        ones = jnp.ones((8, feats), BF16)
        row = dot(ones, shi, ((1,), (1,))) + dot(ones, slo, ((1,), (1,)))
        inv = lax.rsqrt(jnp.maximum(row, TINY))
        p0 = inv.astype(BF16)
        rest = inv - p0.astype(F32)
        p1 = rest.astype(BF16)
        p2 = (rest - p1.astype(F32)).astype(BF16)
        wide = jnp.zeros((8, ref.shape[1] - half), BF16)
        if wide.shape[1]:
            p0, p1, p2 = (jnp.concatenate([p, wide], 1) for p in (p0, p1, p2))
        ref[half : half + 8, :] = p0
        ref[half + 8 : half + 16, :] = p1
        ref[half + 16 : half + 24, :] = p2
        ref[half + 24 : half + 32, :] = jnp.zeros_like(p0)


def listed(lists_ref, row, value):
    hit = lists_ref[row, 0] == value
    for s in range(1, lists_ref.shape[1]):
        hit = jnp.logical_or(hit, lists_ref[row, s] == value)
    return hit


def near_kernel(masks, jobs, first, last, *refs):
    count = len(masks)
    sides = 1 + max(t for t, _ in jobs)
    flat_ref, lists_ref = refs[:2]
    targets = refs[2 : 2 + sides]
    packs = refs[2 + sides : 2 + sides + count]
    x_ref, p_ref, n_ref, acc_ref, todo_ref, x_sem, p_sem = refs[-7:]
    outs = refs[-7 - (2 if last else 1) : -7]
    flat = flat_ref[0]
    size, feats = targets[0].shape
    half = size // 2
    width = outs[0].shape[-1]
    tile = 128
    if not last:
        acc_ref = outs[0]
    hits = [listed(lists_ref, flat ^ t, flat ^ masks[k]).astype(jnp.int32) for t, k in jobs]
    for i, (t, k) in enumerate(jobs):
        todo_ref[0, i] = hits[i]
        todo_ref[1, i] = jnp.int32(t)
        todo_ref[2, i] = jnp.int32(k)
    moves = []
    for t in range(sides):
        need = sum(hit for hit, job in zip(hits, jobs) if job[0] == t)
        moves.append((need, pltpu.make_async_copy(targets[t], x_ref.at[t], x_sem.at[t])))
    for k in range(count):
        need = sum(hit for hit, job in zip(hits, jobs) if job[1] == k)
        moves.append((need, pltpu.make_async_copy(packs[k], p_ref.at[k], p_sem.at[k])))
    for i, (t, k) in enumerate(jobs):
        fresh = hits[i]
        for before, job in zip(hits[:i], jobs[:i]):
            if job[1] == k:
                fresh = fresh * (1 - before)
        todo_ref[3, i] = fresh
    for need, move in moves:
        pl.when(need > 0)(move.start)
    acc_ref[...] = jnp.zeros_like(acc_ref) if first else refs[2 + sides + count][...]

    def job(index, carry):
        active = todo_ref[0, index] > 0
        t = todo_ref[1, index]
        k = todo_ref[2, index]

        for side in range(sides):
            pl.when(active & (carry != t) & (t == side))(moves[side][1].wait)
        for pack in range(count):
            pl.when((todo_ref[3, index] > 0) & (k == pack))(moves[sides + pack][1].wait)

        @pl.when(jnp.logical_and(active, carry != t))
        def _():
            for i in range(size // 256):
                at = pl.ds(i * 256, 256)
                length, inv = norms(x_ref[t, at, :])
                n_ref[0, at, :] = length
                n_ref[1, at, :] = inv

        @pl.when(active)
        def _():
            inv_row = (
                p_ref[k, half : half + 8, 0:half].astype(F32)
                + p_ref[k, half + 8 : half + 16, 0:half].astype(F32)
                + p_ref[k, half + 16 : half + 24, 0:half].astype(F32)
            )[0:1, :]
            weights = p_ref[k, 0:half, feats : feats + 2 * width]
            for i in range(size // tile):
                at = pl.ds(i * tile, tile)
                c = dot(x_ref[t, at, :], p_ref[k, 0:half, 0:feats], ((1,), (1,)))
                hi, lo = halves(unit_kernel(c * n_ref[1, at, :] * inv_row))
                total = dot(hi, weights) + dot(lo, weights)
                acc_ref[t, at, :] += n_ref[0, at, :] * (total[:, 0:width] + total[:, width:])

        return jnp.where(active, t, carry)

    lax.fori_loop(0, len(jobs), job, -1)
    if last:
        outs[0][...] = acc_ref[0]
        outs[1][...] = acc_ref[1]


def basis_kernel(
    basis_hbm, w_hbm, first_hbm, perm_ref, turned_ref, part_ref, hot_ref, basis_ref, w_ref,
    first_ref, sem
):
    moves = []
    for k, (src, dst) in enumerate(
        ((basis_hbm, basis_ref), (w_hbm, w_ref), (first_hbm, first_ref))
    ):
        moves.append(pltpu.make_async_copy(src, dst, sem.at[k]))
        moves[k].start()
    size = basis_ref.shape[1]
    rank = basis_ref.shape[0]
    width = w_ref.shape[1]
    place = lax.rem(perm_ref[...], size)
    for i in range(size // 256):
        spot = lax.broadcasted_iota(jnp.int32, (256, size), 0) + i * 256
        hot_ref[i * 256 : (i + 1) * 256, :] = jnp.where(spot == place, 1.0, 0.0).astype(BF16)
    for move in moves:
        move.wait()
    hi, lo = halves(basis_ref[...])
    pair = jnp.concatenate([hi, lo], 0)
    hot = hot_ref[...]
    turned_ref[...] = dot(hot, pair, ((1,), (1,))).astype(BF16)
    moved = dot(pair, hot, ((1,), (1,))).astype(BF16)
    whi, wlo = halves(w_ref[...])
    y = dot(moved, jnp.concatenate([whi, wlo], 1))
    y = y[0:rank, 0:width] + y[0:rank, width:] + y[rank:, 0:width]
    part_ref[...] = three(first_ref[...], y, ((0,), (0,)))


def climb_kernel(flat_ref, part_ref, *refs):
    pairs, quads = refs[0:2], refs[2:6]
    keep_ref, send_ref, a_ref, b_ref = refs[6:]
    flat = flat_ref[0]
    half, quarter = pairs[0].shape[0], quads[0].shape[0]
    parity = flat % 2
    a_ref[...] = part_ref[...]
    total = None
    for k, ref in enumerate(pairs):
        at = pl.ds(pl.multiple_of((parity ^ k) * half, half), half)
        term = three(ref[...], a_ref[at, :], ((0,), (0,)))
        total = term if total is None else total + term
    b_ref[...] = total
    total = None
    for k, ref in enumerate(quads):
        at = pl.ds(pl.multiple_of(((flat % 4) ^ k) * quarter, quarter), quarter)
        term = three(ref[...], b_ref[at, :], ((0,), (0,)))
        total = term if total is None else total + term
    a_ref[...] = total
    keep_ref[...] = a_ref[pl.ds(pl.multiple_of(parity * half, half), half), :]
    send_ref[...] = a_ref[pl.ds(pl.multiple_of((1 - parity) * half, half), half), :]


def mate_sum_kernel(keep_ref, got_ref, pts_ref, out_ref):
    hi, lo = halves(keep_ref[...] + got_ref[...])
    half, width = keep_ref.shape
    out_ref[0:half, 0:width] = hi
    out_ref[0:half, width:] = lo
    out_ref[half:, :] = pts_ref[...]


def node_sum_kernel(*refs):
    ins, out_ref = refs[:-1], refs[-1]
    rows = (out_ref.shape[0] - ins[0].shape[0]) // (len(ins) - 1)
    half = ins[0].shape[0] - rows
    width = ins[0].shape[1] // 2
    total = None
    for k, ref in enumerate(ins):
        term = ref[0:half, 0:width].astype(F32) + ref[0:half, width:].astype(F32)
        total = term if total is None else total + term
        out_ref[half + k * rows : half + (k + 1) * rows, :] = ref[half:, :]
    hi, lo = halves(total)
    out_ref[0:half, 0:width] = hi
    out_ref[0:half, width:] = lo


def far_kernel(nodes, flat_ref, lists_ref, own_ref, mate_ref, b1_ref, *refs):
    pairs, quads = refs[0:2], refs[2:6]
    turned_ref, out_ref, pts_ref, w_ref, a_ref, b_ref = refs[6:]
    flat = flat_ref[0]
    rank = b1_ref.shape[1]
    half, quarter = pairs[0].shape[0], quads[0].shape[0]
    node, position, parity = flat // NODE, flat % NODE, flat % 2
    width = out_ref.shape[1]
    rows = rank // NODE
    for k, ref in enumerate((own_ref, mate_ref)):
        for m in range(nodes):
            at = (node ^ m) * rank + (parity ^ k) * half
            w_ref[pl.ds(pl.multiple_of(at, half), half), :] = ref[m, 0:half, :]
            for r in range(NODE // 2):
                at = (node ^ m) * rank + (position ^ (2 * r) ^ k) * rows
                low = half + r * rows
                pts_ref[pl.ds(pl.multiple_of(at, rows), rows), :] = ref[m, low : low + rows, :]
    feats = pts_ref.shape[1]
    left = pts_ref[pl.ds(pl.multiple_of(node * rank, rank), rank), :]
    length, inv = norms(left)
    up = jnp.zeros((rank, 2 * width), F32)
    for m in range(nodes):
        at = pl.ds(m * rank, rank)
        pts = pts_ref[at, :]
        wide = pts.astype(F32)
        shi, slo = halves(wide * wide)
        ones = jnp.ones((8, feats), BF16)
        row = dot(ones, shi, ((1,), (1,))) + dot(ones, slo, ((1,), (1,)))
        square = jnp.maximum(row[0:1, :], TINY)
        back = lax.rsqrt(square)
        c = dot(left, pts, ((1,), (1,)))
        scale = jnp.where(listed(lists_ref, node, m), 0.5, 0.0)
        hi, lo = halves(unit_kernel(c * inv * back) * (square * back * scale))
        up = up + dot(hi, w_ref[at, :]) + dot(lo, w_ref[at, :])
    up = length * (up[:, 0:width] + up[:, width:])
    for k, ref in enumerate(quads):
        at = pl.ds(pl.multiple_of(((flat % 4) ^ k) * quarter, quarter), quarter)
        a_ref[at, :] = three(ref[...], up)
    up = a_ref[...]
    for k, ref in enumerate(pairs):
        at = pl.ds(pl.multiple_of((parity ^ k) * half, half), half)
        b_ref[at, :] = three(ref[...], up)
    up = three(b1_ref[...], b_ref[...])
    hi, lo = halves(up)
    top = jnp.concatenate([hi, lo], 1)
    low = jnp.concatenate([hi, jnp.zeros_like(lo)], 1)
    far = dot(turned_ref[...], jnp.concatenate([top, low], 0))
    out_ref[...] = far[:, 0:width] + far[:, width:]


def join_kernel(a_ref, b_ref, c_ref, out_ref):
    out_ref[...] = (a_ref[...] + c_ref[...]) + b_ref[...]


def stack_kernel(*refs):
    for k, ref in enumerate(refs[:-1]):
        refs[-1][k] = ref[...]


def body(
    points, rhs, permutation, leaf_basis, climb_leaf, climb_pair, climb_quad, skel_points,
    near_lists, far_lists
):
    size, feats = points.shape
    width = rhs.shape[1]
    rank = climb_leaf.shape[1]
    nodes = lax.axis_size(AXES) // NODE
    flat = lax.axis_index(AXES).astype(jnp.int32).reshape(1)
    struct = jax.ShapeDtypeStruct

    quads = [climb_quad] + [across(climb_quad, k) for k in (1, 2, 3)]
    pairs = [climb_pair, across(climb_pair, 1)]

    mate_pts = across(points, 1)
    pack_shape = struct((size // 2 + 32, max(feats + 2 * width, size // 2)), BF16)
    pack_a, pack_b = call(
        pack_kernel, [pack_shape, pack_shape], 0, (points, rhs),
        [
            pltpu.VMEM((size, feats), BF16),
            pltpu.VMEM((size, width), F32),
            pltpu.SemaphoreType.DMA((4,)),
        ],
        loose=2,
        far_memory=True,
    )
    x_a, y_a = across(pack_a, 2), across(pack_a, 4)
    x_b, y_b = across(pack_b, 2), across(pack_b, 4)
    d_a = across(y_a, 2)
    d_b = across(x_b, 4)
    masks = [NODE * m for m in range(1, nodes)]

    block = 2 * size * size * (feats + 6 * width) * 4
    sums = struct((size, width), F32)

    def near(masks, jobs, packs, before=None, last=False):
        kernel = functools.partial(near_kernel, masks, jobs, before is None, last)
        before = () if before is None else (before,)
        sides = (points, mate_pts)[: 1 + max(t for t, _ in jobs)]
        loose = len(sides) + len(masks)
        return call(
            kernel, [sums, sums] if last else struct((2, size, width), F32), 2,
            (flat, near_lists, *sides, *packs, *before),
            [
                pltpu.VMEM((len(sides), size, feats), BF16),
                pltpu.VMEM((len(masks), *pack_shape.shape), BF16),
                pltpu.VMEM((2, size, 1), F32),
                pltpu.VMEM((2, size, width) if last else (8, 128), F32),
                pltpu.SMEM((4, len(jobs)), jnp.int32),
                pltpu.SemaphoreType.DMA((len(sides),)),
                pltpu.SemaphoreType.DMA((len(masks),)),
            ],
            flops=block * len(jobs) // 2,
            loose=loose,
        )

    turned, part = call(
        basis_kernel,
        [struct((size, 2 * rank), BF16), struct((rank, width), F32)],
        0,
        (leaf_basis, rhs, climb_leaf, permutation.reshape(1, size)),
        [
            pltpu.VMEM((size, size), BF16),
            pltpu.VMEM((rank, size), F32),
            pltpu.VMEM((size, width), F32),
            pltpu.VMEM((rank, rank), F32),
            pltpu.SemaphoreType.DMA((3,)),
        ],
        loose=3,
        far_memory=True,
        flops=2 * size * size * rank * 6,
    )
    strip = struct((rank // 2, width), F32)
    keep, send = call(
        climb_kernel, [strip, strip], 1, (flat, part, *pairs, *quads),
        [pltpu.VMEM((rank, width), F32), pltpu.VMEM((rank, width), F32)],
        flops=2 * rank * rank * width * 12,
    )
    rows = rank // 2 + skel_points.shape[0]
    strip = call(
        mate_sum_kernel, struct((rows, 2 * width), BF16), 0,
        (keep, across(send, 1), skel_points),
    )
    strips = [strip] + [across(strip, k) for k in (2, 4, 6)]
    rows = rank // 2 + 4 * skel_points.shape[0]
    value = call(node_sum_kernel, struct((rows, 2 * width), BF16), 0, tuple(strips))
    others = [across(value, m) for m in masks]
    every = call(stack_kernel, struct((nodes, *value.shape), BF16), 0, (value, *others))
    every_mate = across(every, 1)

    own = (pack_a, pack_b)
    total = near((0, 0), ((0, 0), (0, 1)), own)
    total = near((0, 0), ((1, 0), (1, 1)), own, total)
    jobs = [(t, k) for t in range(2) for k in range(4)]
    total = near((2, 2, 4, 4), jobs, (x_a, x_b, y_a, y_b), total)
    jobs = ((0, 0), (0, 1), (1, 0), (1, 1))
    mine, other = near((6, 6), jobs, (d_a, d_b), total, True)
    far = call(
        functools.partial(far_kernel, nodes),
        sums,
        2,
        (
            flat, far_lists, every, every_mate, climb_leaf, *pairs, *quads, turned
        ),
        [
            pltpu.VMEM((nodes * rank, feats), BF16),
            pltpu.VMEM((nodes * rank, 2 * width), BF16),
            pltpu.VMEM((rank, width), F32),
            pltpu.VMEM((rank, width), F32),
        ],
        flops=2 * rank * rank * width * 60,
    )
    return call(join_kernel, sums, 0, (mine, across(other, 1), far))


def solution(mesh):
    split = P(AXES, None)

    return jax.shard_map(
        body,
        mesh=mesh,
        in_specs=(split, split, P(AXES), split, split, split, split, split, P(), P()),
        out_specs=split,
        check_vma=False,
    )
```

time: 87.2 us -> 80.6 us (0.924)
  the two profiles are of different devices: /device:TPU:7 before, /device:TPU:9 now
where the time goes in v1:
time: 80.6 us; the launch traced here: 80.2 us
  Pallas kernels  39.3 us (49%)
  starting transfers between devices  20.3 us (25%)
  waiting for transfers between devices  15.3 us (19%)
  local copies, waits for them, and re-layouts  5 us (6%)
    pallas_call x12, Pallas kernels, call(): pl.pallas_call(kernel, out_shape=out, in_specs=specs, out_specs=[pl.Block...  39.3 us
    ppermute x20, starting transfers between devices, across(): return lax.ppermute(value, AXES, pairs)  20.3 us
    ppermute x20, waiting for transfers between devices, across(): return lax.ppermute(value, AXES, pairs)  15.3 us
    unnamed x33, local copies, waits for them, and re-layouts  5 us
  transfers between devices with their start and end apart: 20, of which 5 were waited for; matrix products, arithmetic and copies ran while one was open for 0% of the time, Pallas kernels for 47%

profile of v1, /device:TPU:9, one launch (start us, length us, event | category | flops | bytes accessed | tf_op | source)
XLA Modules:
  0.0 80.2 jit_solution(15982743973461951973)
XLA Ops:
  0.0 1.2 %collective-permute-start.10 = (f32[64,256]{1,0:T(8,128)}, f32[64,256]{1,0:T(8,128)S(1)}, u32[]{:S(2)}, u32[]{:S(2)}) collective-permute-start(f32[64,256]{1,0:T(8,128)} %refs_2_.11), channel_id=1, source_target_pairs={{0,2},{1,3},{2,0},{3,1},{4,6},{5,7},{6,4},{7,5},{8,10},{9,11},{10,... | collective-permute-start | bytes 196616 | tf_op jit(solution)/shard_map/ppermute | solution.py:31
  1.2 1.1 %collective-permute-start.11 = (f32[64,256]{1,0:T(8,128)}, f32[64,256]{1,0:T(8,128)S(1)}, u32[]{:S(2)}, u32[]{:S(2)}) collective-permute-start(f32[64,256]{1,0:T(8,128)} %refs_2_.11), channel_id=1, source_target_pairs={{0,3},{1,2},{2,1},{3,0},{4,7},{5,6},{6,5},{7,4},{8,11},{9,10},{10,... | collective-permute-start | bytes 196616 | tf_op jit(solution)/shard_map/ppermute | solution.py:31
  2.3 0.0 collective-permute-start.9
  2.3 0.5 collective-permute-start.8
  2.8 1.0 %copy-done = f32[1024,128]{1,0:T(8,128)S(1)} copy-done((f32[1024,128]{1,0:T(8,128)S(1)}, f32[1024,128]{1,0:T(8,128)}, u32[]{:S(2)}) %copy-start) | copy-done | bytes 524312
  3.9 1.2 %copy-done.4 = f32[256,1024]{1,0:T(8,128)S(1)} copy-done((f32[256,1024]{1,0:T(8,128)S(1)}, f32[256,1024]{1,0:T(8,128)}, u32[]{:S(2)}) %copy-start.4) | copy-done | bytes 1048600
  5.1 0.9 %copy-done.5 = f32[256,256]{1,0:T(8,128)S(1)} copy-done((f32[256,256]{1,0:T(8,128)S(1)}, f32[256,256]{1,0:T(8,128)}, u32[]{:S(2)}) %copy-start.5) | copy-done | bytes 262168
  6.0 0.7 copy-done.11
  6.7 3.3 %shard_map.105 = (bf16[1024,512]{1,0:T(8,128)(2,1)S(1)}, f32[256,128]{1,0:T(8,128)S(1)}) custom-call(f32[256,1024]{1,0:T(8,128)S(1)} %copy-done.4, f32[1024,128]{1,0:T(8,128)S(1)} %copy-done, f32[256,256]{1,0:T(8,128)S(1)} %copy-done.5, s32[1,1024]{1,0:T(1,128)S(1)} %bitcast.2), custom_call_target="tpu_custom_call" | custom-call | flops 3221225472 | tf_op jit(solution)/shard_map/pallas_call | solution.py:40
  10.0 0.0 copy-start.13
  10.1 1.0 %copy-done.13 = bf16[1024,512]{1,0:T(8,128)(2,1)} copy-done((bf16[1024,512]{1,0:T(8,128)(2,1)}, bf16[1024,512]{1,0:T(8,128)(2,1)S(1)}, u32[]{:S(2)}) %copy-start.13) | copy-done | bytes 1048600
  11.0 0.0 collective-permute-done.10.refs_4_
  11.0 0.0 collective-permute-done.11.refs_5_
  11.0 0.0 collective-permute-done.9.refs_3_
  11.0 0.0 copy-start.9
  11.1 0.0 collective-permute-done.8.refs_1_
  11.1 0.0 copy-start.3
  11.1 0.8 shard_map.106
  11.9 0.1 collective-permute-start.12
  12.0 1.2 %collective-permute-done.12.got_ref = f32[128,128]{1,0:T(8,128)S(1)} collective-permute-done((f32[128,128]{1,0:T(8,128)S(1)}, f32[128,128]{1,0:T(8,128)S(1)}, u32[]{:S(2)}, u32[]{:S(2)}) %collective-permute-start.12) | collective-permute-done | bytes 65568 | tf_op jit(solution)/shard_map/ppermute | solution.py:31
  13.2 1.3 %collective-permute-start.13 = (bf16[160,256]{1,0:T(8,128)(2,1)S(1)}, bf16[160,256]{1,0:T(8,128)(2,1)S(1)}, u32[]{:S(2)}, u32[]{:S(2)}) collective-permute-start(bf16[160,256]{1,0:T(8,128)(2,1)S(1)} %shard_map.107.refs_0_), channel_id=1, source_target_pairs={{0,2},{1,3},{2,0},{3,1},{4,6},{5,7},{6,4},{7,5},{8,10},{9,11},{10,... | collective-permute-start | bytes 245768 | tf_op jit(solution)/shard_map/ppermute | solution.py:31
  14.5 1.2 %collective-permute-start.14 = (bf16[160,256]{1,0:T(8,128)(2,1)S(1)}, bf16[160,256]{1,0:T(8,128)(2,1)S(1)}, u32[]{:S(2)}, u32[]{:S(2)}) collective-permute-start(bf16[160,256]{1,0:T(8,128)(2,1)S(1)} %shard_map.107.refs_0_), channel_id=1, source_target_pairs={{0,4},{1,5},{2,6},{3,7},{4,0},{5,1},{6,2},{7,3},{8,12},{9,13},{10,... | collective-permute-start | bytes 245768 | tf_op jit(solution)/shard_map/ppermute | solution.py:31
  15.7 0.2 collective-permute-start.15
  16.0 1.0 %collective-permute-start = (bf16[1024,256]{1,0:T(8,128)(2,1)S(1)}, bf16[1024,256]{1,0:T(8,128)(2,1)}, u32[]{:S(2)}, u32[]{:S(2)}) collective-permute-start(bf16[1024,256]{1,0:T(8,128)(2,1)S(1)} %copy-done.2), channel_id=1, source_target_pairs={{0,1},{1,0},{2,3},{3,2},{4,5},{5,4},{6,7},{7,6},{8,9},{9,8},{10,11... | collective-permute-start | bytes 1572872 | tf_op jit(solution)/shard_map/ppermute | solution.py:31
  17.0 0.0 copy-done.1
  17.0 0.7 shard_map.100
  17.7 1.3 %collective-permute-start.1 = (bf16[544,512]{1,0:T(8,128)(2,1)S(1)}, bf16[544,512]{1,0:T(8,128)(2,1)S(1)}, u32[]{:S(2)}, u32[]{:S(2)}) collective-permute-start(bf16[544,512]{1,0:T(8,128)(2,1)S(1)} %get-tuple-element.13.refs_3_.refs_4_), channel_id=1, source_target_pairs={{0,4},{1,5},{2,6},{3,7},{4,0},{5,1},{6,2},{7,3},{8,12},{9,13},{10,... | collective-permute-start | bytes 1671176 | tf_op jit(solution)/shard_map/ppermute | solution.py:31
  19.0 0.0 copy-done.15
  19.0 0.1 copy.14.refs_1_
  19.1 0.0 collective-permute-done.13.refs_1_
  19.1 0.0 collective-permute-done.14.refs_2_
  19.1 0.9 %collective-permute-done.15.refs_3_ = bf16[160,256]{1,0:T(8,128)(2,1)S(1)} collective-permute-done((bf16[160,256]{1,0:T(8,128)(2,1)S(1)}, bf16[160,256]{1,0:T(8,128)(2,1)S(1)}, u32[]{:S(2)}, u32[]{:S(2)}) %collective-permute-start.15) | collective-permute-done | bytes 81952 | tf_op jit(solution)/shard_map/ppermute | solution.py:31
  20.0 0.2 collective-permute-start.16
  20.2 2.3 %collective-permute-start.17 = (bf16[256,256]{1,0:T(8,128)(2,1)S(1)}, bf16[256,256]{1,0:T(8,128)(2,1)S(1)}, u32[]{:S(2)}, u32[]{:S(2)}) collective-permute-start(bf16[256,256]{1,0:T(8,128)(2,1)S(1)} %shard_map.108.refs_0_), channel_id=1, source_target_pairs={{0,16},{1,17},{2,18},{3,19},{4,20},{5,21},{6,22},{7,23},{8,24},{9,... | collective-permute-start | bytes 393224 | tf_op jit(solution)/shard_map/ppermute | solution.py:31
  22.5 0.2 collective-permute-start.18
  22.7 5.7 %shard_map.101.refs_6_ = f32[2,1024,128]{2,1,0:T(8,128)S(1)} custom-call(s32[1]{0:T(128)} %bitcast.refs_0_.flat_ref, s32[32,8]{1,0:T(8,128)S(1)} %copy.14.refs_1_, bf16[1024,256]{1,0:T(8,128)(2,1)S(1)} %copy-done.2, bf16[544,512]{1,0:T(8,128)(2,1)S(1)} %get-tuple-element.13.refs_3_.refs_4_, bf16[544,512]{1,0:T(8,128)(2,1)S(1)} %get-tuple-element.14.refs_4_.refs_5_), custom_call_target="tpu_custom_call" | custom-call | flops 8589934592 | tf_op jit(solution)/shard_map/pallas_call | solution.py:40
  28.5 0.0 collective-permute-done.16.refs_1_
  28.5 0.9 %collective-permute-start.3 = (bf16[544,512]{1,0:T(8,128)(2,1)S(1)}, bf16[544,512]{1,0:T(8,128)(2,1)S(1)}, u32[]{:S(2)}, u32[]{:S(2)}) collective-permute-start(bf16[544,512]{1,0:T(8,128)(2,1)S(1)} %get-tuple-element.14.refs_4_.refs_5_), channel_id=1, source_target_pairs={{0,2},{1,3},{2,0},{3,1},{4,6},{5,7},{6,4},{7,5},{8,10},{9,11},{10,... | collective-permute-start | bytes 1671176 | tf_op jit(solution)/shard_map/ppermute | solution.py:31
  29.4 0.0 collective-permute-done.17.refs_2_
  29.4 0.6 collective-permute-start.5
  30.0 3.4 %collective-permute-done.18.refs_3_ = bf16[256,256]{1,0:T(8,128)(2,1)S(1)} collective-permute-done((bf16[256,256]{1,0:T(8,128)(2,1)S(1)}, bf16[256,256]{1,0:T(8,128)(2,1)S(1)}, u32[]{:S(2)}, u32[]{:S(2)}) %collective-permute-start.18) | collective-permute-done | bytes 131104 | tf_op jit(solution)/shard_map/ppermute | solution.py:31
  33.4 0.4 collective-permute-start.6
  33.8 0.0 collective-permute-done.refs_3_
  33.8 2.5 %collective-permute-start.19 = (bf16[4,256,256]{2,1,0:T(8,128)(2,1)S(1)}, bf16[4,256,256]{2,1,0:T(8,128)(2,1)S(1)}, u32[]{:S(2)}, u32[]{:S(2)}) collective-permute-start(bf16[4,256,256]{2,1,0:T(8,128)(2,1)S(1)} %shard_map.109.own_ref), channel_id=1, source_target_pairs={{0,1},{1,0},{2,3},{3,2},{4,5},{5,4},{6,7},{7,6},{8,9},{9,8},{10,11... | collective-permute-start | bytes 1572872 | tf_op jit(solution)/shard_map/ppermute | solution.py:31
  36.3 6.5 %shard_map.102.refs_8_ = f32[2,1024,128]{2,1,0:T(8,128)S(1)} custom-call(s32[1]{0:T(128)} %bitcast.refs_0_.flat_ref, s32[32,8]{1,0:T(8,128)S(1)} %copy.14.refs_1_, bf16[1024,256]{1,0:T(8,128)(2,1)S(1)} %copy-done.2, bf16[1024,256]{1,0:T(8,128)(2,1)} %collective-permute-done.refs_3_, bf16[544,512]{1,0:T(8,128)(2,1)S(1)} %get-tuple-element.13.refs_3_.refs_4_, ...), custom_call_target="tpu_custom_call" | custom-call | flops 8589934592 | tf_op jit(solution)/shard_map/pallas_call | solution.py:40
  42.8 0.0 collective-permute-done.1.refs_6_
  42.8 0.1 collective-permute-start.2
  42.9 0.0 collective-permute-done.3.refs_5_
  42.9 0.1 collective-permute-start.4
  43.0 8.8 %collective-permute-done.5.refs_4_ = bf16[544,512]{1,0:T(8,128)(2,1)S(1)} collective-permute-done((bf16[544,512]{1,0:T(8,128)(2,1)S(1)}, bf16[544,512]{1,0:T(8,128)(2,1)S(1)}, u32[]{:S(2)}, u32[]{:S(2)}) %collective-permute-start.5) | collective-permute-done | bytes 557088 | tf_op jit(solution)/shard_map/ppermute | solution.py:31
  51.8 0.0 collective-permute-done.6.refs_7_
  51.8 11.0 %shard_map.103.refs_6_ = f32[2,1024,128]{2,1,0:T(8,128)S(1)} custom-call(s32[1]{0:T(128)} %bitcast.refs_0_.flat_ref, s32[32,8]{1,0:T(8,128)S(1)} %copy.14.refs_1_, bf16[1024,256]{1,0:T(8,128)(2,1)S(1)} %copy-done.2, bf16[1024,256]{1,0:T(8,128)(2,1)} %collective-permute-done.refs_3_, bf16[544,512]{1,0:T(8,128)(2,1)S(1)} %collective-permute-done.5.refs_4_, ...), custom_call_target="tpu_custom_call" | custom-call | flops 34359738368 | tf_op jit(solution)/shard_map/pallas_call | solution.py:40
  62.8 0.0 copy-start.6
  62.9 0.0 copy-start.10
  62.9 0.9 %collective-permute-done.2.refs_4_ = bf16[544,512]{1,0:T(8,128)(2,1)S(1)} collective-permute-done((bf16[544,512]{1,0:T(8,128)(2,1)S(1)}, bf16[544,512]{1,0:T(8,128)(2,1)S(1)}, u32[]{:S(2)}, u32[]{:S(2)}) %collective-permute-start.2) | collective-permute-done | bytes 557088 | tf_op jit(solution)/shard_map/ppermute | solution.py:31
  63.8 0.0 collective-permute-done.4.refs_5_
  63.8 6.6 %shard_map.104 = (f32[1024,128]{1,0:T(8,128)S(1)}, f32[1024,128]{1,0:T(8,128)S(1)}) custom-call(s32[1]{0:T(128)} %bitcast.refs_0_.flat_ref, s32[32,8]{1,0:T(8,128)S(1)} %copy.14.refs_1_, bf16[1024,256]{1,0:T(8,128)(2,1)S(1)} %copy-done.2, bf16[1024,256]{1,0:T(8,128)(2,1)} %collective-permute-done.refs_3_, ...), custom_call_target="tpu_custom_call" | custom-call | flops 17179869184 | tf_op jit(solution)/shard_map/pallas_call | solution.py:40
  70.4 0.0 copy-start.12
  70.4 5.2 %collective-permute-start.7 = (f32[1024,128]{1,0:T(8,128)S(1)}, f32[1024,128]{1,0:T(8,128)S(1)}, u32[]{:S(2)}, u32[]{:S(2)}) collective-permute-start(f32[1024,128]{1,0:T(8,128)S(1)} %get-tuple-element.16), channel_id=1, source_target_pairs={{0,1},{1,0},{2,3},{3,2},{4,5},{5,4},{6,7},{7,6},{8,9},{9,8},{10,11... | collective-permute-start | bytes 1572872 | tf_op jit(solution)/shard_map/ppermute | solution.py:31
  75.5 0.0 collective-permute-done.19.mate_ref
  75.5 0.0 copy-done.6
  75.6 3.8 %shard_map.110.c_ref = f32[1024,128]{1,0:T(8,128)S(1)} custom-call(s32[1]{0:T(128)} %bitcast.refs_0_.flat_ref, s32[4,3]{1,0:T(4,128)S(1)} %copy-done.12, bf16[4,256,256]{2,1,0:T(8,128)(2,1)S(1)} %shard_map.109.own_ref, bf16[4,256,256]{2,1,0:T(8,128)(2,1)S(1)} %collective-permute-done.19.mate_ref, f32[256,256]{1,0:T(8,128)S(1)} %copy-done.6, ...), custom_call_target="tpu_custom_call" | custom-call | flops 1006632960 | tf_op jit(solution)/shard_map/pallas_call | solution.py:40
  79.3 0.0 collective-permute-done.7.b_ref
  79.3 0.9 %shard_map.111 = f32[1024,128]{1,0:T(8,128)} custom-call(f32[1024,128]{1,0:T(8,128)S(1)} %get-tuple-element.15.a_ref, f32[1024,128]{1,0:T(8,128)S(1)} %collective-permute-done.7.b_ref, f32[1024,128]{1,0:T(8,128)S(1)} %shard_map.110.c_ref), custom_call_target="tpu_custom_call" | custom-call | tf_op jit(solution)/shard_map/pallas_call | solution.py:40
  (21 shorter events, 0.1 us)
Async XLA Ops:
  0.0 11.0 %collective-permute-start.10 = (f32[64,256]{1,0:T(8,128)}, f32[64,256]{1,0:T(8,128)S(1)}, u32[]{:S(2)}, u32[]{:S(2)}) collective-permute-start(f32[64,256]{1,0:T(8,128)} %refs_2_.11), channel_id=1, source_target_pairs={{0,2},{1,3},{2,0},{3,1},{4,6},{5,7},{6,4},{7,5},{8,10},{9,11},{10,... | collective-permute-start | bytes 196616 | tf_op jit(solution)/shard_map/ppermute | solution.py:31
  1.2 9.8 %collective-permute-start.11 = (f32[64,256]{1,0:T(8,128)}, f32[64,256]{1,0:T(8,128)S(1)}, u32[]{:S(2)}, u32[]{:S(2)}) collective-permute-start(f32[64,256]{1,0:T(8,128)} %refs_2_.11), channel_id=1, source_target_pairs={{0,3},{1,2},{2,1},{3,0},{4,7},{5,6},{6,5},{7,4},{8,11},{9,10},{10,... | collective-permute-start | bytes 196616 | tf_op jit(solution)/shard_map/ppermute | solution.py:31
  2.3 8.7 %collective-permute-start.9 = (f32[64,256]{1,0:T(8,128)}, f32[64,256]{1,0:T(8,128)S(1)}, u32[]{:S(2)}, u32[]{:S(2)}) collective-permute-start(f32[64,256]{1,0:T(8,128)} %refs_2_.11), channel_id=1, source_target_pairs={{0,1},{1,0},{2,3},{3,2},{4,5},{5,4},{6,7},{7,6},{8,9},{9,8},{10,11... | collective-permute-start | bytes 196616 | tf_op jit(solution)/shard_map/ppermute | solution.py:31
  2.3 8.7 %collective-permute-start.8 = (f32[128,256]{1,0:T(8,128)}, f32[128,256]{1,0:T(8,128)S(1)}, u32[]{:S(2)}, u32[]{:S(2)}) collective-permute-start(f32[128,256]{1,0:T(8,128)} %refs_0_.3), channel_id=1, source_target_pairs={{0,1},{1,0},{2,3},{3,2},{4,5},{5,4},{6,7},{7,6},{8,9},{9,8},{10,11... | collective-permute-start | bytes 393224 | tf_op jit(solution)/shard_map/ppermute | solution.py:31
  2.8 1.0 %copy-start = (f32[1024,128]{1,0:T(8,128)S(1)}, f32[1024,128]{1,0:T(8,128)}, u32[]{:S(2)}) copy-start(f32[1024,128]{1,0:T(8,128)} %w_hbm.3) | copy-start | bytes 1572868
  3.9 1.2 %copy-start.4 = (f32[256,1024]{1,0:T(8,128)S(1)}, f32[256,1024]{1,0:T(8,128)}, u32[]{:S(2)}) copy-start(f32[256,1024]{1,0:T(8,128)} %basis_hbm.1) | copy-start | bytes 3145732
  5.1 0.9 %copy-start.5 = (f32[256,256]{1,0:T(8,128)S(1)}, f32[256,256]{1,0:T(8,128)}, u32[]{:S(2)}) copy-start(f32[256,256]{1,0:T(8,128)} %b1_ref.1) | copy-start | bytes 786436
  6.0 0.7 copy-start.11
  6.7 4.3 %copy-start.7 = (f32[128,256]{1,0:T(8,128)S(1)}, f32[128,256]{1,0:T(8,128)}, u32[]{:S(2)}) copy-start(f32[128,256]{1,0:T(8,128)} %refs_0_.3) | copy-start | bytes 393220
  6.7 4.4 %copy-start.8 = (f32[64,256]{1,0:T(8,128)S(1)}, f32[64,256]{1,0:T(8,128)}, u32[]{:S(2)}) copy-start(f32[64,256]{1,0:T(8,128)} %refs_2_.11) | copy-start | bytes 196612
  6.7 9.2 %copy-start.2 = (bf16[1024,256]{1,0:T(8,128)(2,1)S(1)}, bf16[1024,256]{1,0:T(8,128)(2,1)}, u32[]{:S(2)}) copy-start(bf16[1024,256]{1,0:T(8,128)(2,1)} %refs_2_.9) | copy-start | bytes 1572868
  10.0 1.0 %copy-start.13 = (bf16[1024,512]{1,0:T(8,128)(2,1)}, bf16[1024,512]{1,0:T(8,128)(2,1)S(1)}, u32[]{:S(2)}) copy-start(bf16[1024,512]{1,0:T(8,128)(2,1)S(1)} %get-tuple-element.20.refs_6_) | copy-start | bytes 3145732
  11.0 5.9 %copy-start.1 = (f32[1024,128]{1,0:T(8,128)S(1)}, f32[1024,128]{1,0:T(8,128)}, u32[]{:S(2)}) copy-start(f32[1024,128]{1,0:T(8,128)} %w_hbm.3) | copy-start | bytes 1572868
  11.0 0.8 %copy-start.9 = (f32[64,256]{1,0:T(8,128)}, f32[64,256]{1,0:T(8,128)S(1)}, u32[]{:S(2)}) copy-start(f32[64,256]{1,0:T(8,128)S(1)} %collective-permute-done.9.refs_3_) | copy-start | bytes 196612
  11.1 2.1 %copy-start.3 = (bf16[32,256]{1,0:T(8,128)(2,1)S(1)}, bf16[32,256]{1,0:T(8,128)(2,1)}, u32[]{:S(2)}) copy-start(bf16[32,256]{1,0:T(8,128)(2,1)} %pts_ref.1) | copy-start | bytes 49156
  11.9 1.3 %collective-permute-start.12 = (f32[128,128]{1,0:T(8,128)S(1)}, f32[128,128]{1,0:T(8,128)S(1)}, u32[]{:S(2)}, u32[]{:S(2)}) collective-permute-start(f32[128,128]{1,0:T(8,128)S(1)} %get-tuple-element.19), channel_id=1, source_target_pairs={{0,1},{1,0},{2,3},{3,2},{4,5},{5,4},{6,7},{7,6},{8,9},{9,8},{10,11... | collective-permute-start | bytes 196616 | tf_op jit(solution)/shard_map/ppermute | solution.py:31
  13.2 5.8 %collective-permute-start.13 = (bf16[160,256]{1,0:T(8,128)(2,1)S(1)}, bf16[160,256]{1,0:T(8,128)(2,1)S(1)}, u32[]{:S(2)}, u32[]{:S(2)}) collective-permute-start(bf16[160,256]{1,0:T(8,128)(2,1)S(1)} %shard_map.107.refs_0_), channel_id=1, source_target_pairs={{0,2},{1,3},{2,0},{3,1},{4,6},{5,7},{6,4},{7,5},{8,10},{9,11},{10,... | collective-permute-start | bytes 245768 | tf_op jit(solution)/shard_map/ppermute | solution.py:31
  14.5 4.6 %collective-permute-start.14 = (bf16[160,256]{1,0:T(8,128)(2,1)S(1)}, bf16[160,256]{1,0:T(8,128)(2,1)S(1)}, u32[]{:S(2)}, u32[]{:S(2)}) collective-permute-start(bf16[160,256]{1,0:T(8,128)(2,1)S(1)} %shard_map.107.refs_0_), channel_id=1, source_target_pairs={{0,4},{1,5},{2,6},{3,7},{4,0},{5,1},{6,2},{7,3},{8,12},{9,13},{10,... | collective-permute-start | bytes 245768 | tf_op jit(solution)/shard_map/ppermute | solution.py:31
  15.7 4.2 %collective-permute-start.15 = (bf16[160,256]{1,0:T(8,128)(2,1)S(1)}, bf16[160,256]{1,0:T(8,128)(2,1)S(1)}, u32[]{:S(2)}, u32[]{:S(2)}) collective-permute-start(bf16[160,256]{1,0:T(8,128)(2,1)S(1)} %shard_map.107.refs_0_), channel_id=1, source_target_pairs={{0,6},{1,7},{2,4},{3,5},{4,2},{5,3},{6,0},{7,1},{8,14},{9,15},{10,... | collective-permute-start | bytes 245768 | tf_op jit(solution)/shard_map/ppermute | solution.py:31
  16.0 17.8 %collective-permute-start = (bf16[1024,256]{1,0:T(8,128)(2,1)S(1)}, bf16[1024,256]{1,0:T(8,128)(2,1)}, u32[]{:S(2)}, u32[]{:S(2)}) collective-permute-start(bf16[1024,256]{1,0:T(8,128)(2,1)S(1)} %copy-done.2), channel_id=1, source_target_pairs={{0,1},{1,0},{2,3},{3,2},{4,5},{5,4},{6,7},{7,6},{8,9},{9,8},{10,11... | collective-permute-start | bytes 1572872 | tf_op jit(solution)/shard_map/ppermute | solution.py:31
  17.0 2.0 %copy-start.15 = (s32[32,8]{0,1:T(8,128)S(1)}, s32[32,8]{0,1:T(8,128)}, u32[]{:S(2)}) copy-start(s32[32,8]{0,1:T(8,128)} %param.18) | copy-start | bytes 3076
  17.7 25.1 %collective-permute-start.1 = (bf16[544,512]{1,0:T(8,128)(2,1)S(1)}, bf16[544,512]{1,0:T(8,128)(2,1)S(1)}, u32[]{:S(2)}, u32[]{:S(2)}) collective-permute-start(bf16[544,512]{1,0:T(8,128)(2,1)S(1)} %get-tuple-element.13.refs_3_.refs_4_), channel_id=1, source_target_pairs={{0,4},{1,5},{2,6},{3,7},{4,0},{5,1},{6,2},{7,3},{8,12},{9,13},{10,... | collective-permute-start | bytes 1671176 | tf_op jit(solution)/shard_map/ppermute | solution.py:31
  20.0 8.5 %collective-permute-start.16 = (bf16[256,256]{1,0:T(8,128)(2,1)S(1)}, bf16[256,256]{1,0:T(8,128)(2,1)S(1)}, u32[]{:S(2)}, u32[]{:S(2)}) collective-permute-start(bf16[256,256]{1,0:T(8,128)(2,1)S(1)} %shard_map.108.refs_0_), channel_id=1, source_target_pairs={{0,8},{1,9},{2,10},{3,11},{4,12},{5,13},{6,14},{7,15},{8,0},{9,1},... | collective-permute-start | bytes 393224 | tf_op jit(solution)/shard_map/ppermute | solution.py:31
  20.2 9.2 %collective-permute-start.17 = (bf16[256,256]{1,0:T(8,128)(2,1)S(1)}, bf16[256,256]{1,0:T(8,128)(2,1)S(1)}, u32[]{:S(2)}, u32[]{:S(2)}) collective-permute-start(bf16[256,256]{1,0:T(8,128)(2,1)S(1)} %shard_map.108.refs_0_), channel_id=1, source_target_pairs={{0,16},{1,17},{2,18},{3,19},{4,20},{5,21},{6,22},{7,23},{8,24},{9,... | collective-permute-start | bytes 393224 | tf_op jit(solution)/shard_map/ppermute | solution.py:31
  22.5 10.8 %collective-permute-start.18 = (bf16[256,256]{1,0:T(8,128)(2,1)S(1)}, bf16[256,256]{1,0:T(8,128)(2,1)S(1)}, u32[]{:S(2)}, u32[]{:S(2)}) collective-permute-start(bf16[256,256]{1,0:T(8,128)(2,1)S(1)} %shard_map.108.refs_0_), channel_id=1, source_target_pairs={{0,24},{1,25},{2,26},{3,27},{4,28},{5,29},{6,30},{7,31},{8,16},{9,... | collective-permute-start | bytes 393224 | tf_op jit(solution)/shard_map/ppermute | solution.py:31
  28.5 14.4 %collective-permute-start.3 = (bf16[544,512]{1,0:T(8,128)(2,1)S(1)}, bf16[544,512]{1,0:T(8,128)(2,1)S(1)}, u32[]{:S(2)}, u32[]{:S(2)}) collective-permute-start(bf16[544,512]{1,0:T(8,128)(2,1)S(1)} %get-tuple-element.14.refs_4_.refs_5_), channel_id=1, source_target_pairs={{0,2},{1,3},{2,0},{3,1},{4,6},{5,7},{6,4},{7,5},{8,10},{9,11},{10,... | collective-permute-start | bytes 1671176 | tf_op jit(solution)/shard_map/ppermute | solution.py:31
  29.4 22.4 %collective-permute-start.5 = (bf16[544,512]{1,0:T(8,128)(2,1)S(1)}, bf16[544,512]{1,0:T(8,128)(2,1)S(1)}, u32[]{:S(2)}, u32[]{:S(2)}) collective-permute-start(bf16[544,512]{1,0:T(8,128)(2,1)S(1)} %get-tuple-element.13.refs_3_.refs_4_), channel_id=1, source_target_pairs={{0,2},{1,3},{2,0},{3,1},{4,6},{5,7},{6,4},{7,5},{8,10},{9,11},{10,... | collective-permute-start | bytes 1671176 | tf_op jit(solution)/shard_map/ppermute | solution.py:31
  33.4 18.5 %collective-permute-start.6 = (bf16[544,512]{1,0:T(8,128)(2,1)S(1)}, bf16[544,512]{1,0:T(8,128)(2,1)S(1)}, u32[]{:S(2)}, u32[]{:S(2)}) collective-permute-start(bf16[544,512]{1,0:T(8,128)(2,1)S(1)} %get-tuple-element.14.refs_4_.refs_5_), channel_id=1, source_target_pairs={{0,4},{1,5},{2,6},{3,7},{4,0},{5,1},{6,2},{7,3},{8,12},{9,13},{10,... | collective-permute-start | bytes 1671176 | tf_op jit(solution)/shard_map/ppermute | solution.py:31
  33.8 41.7 %collective-permute-start.19 = (bf16[4,256,256]{2,1,0:T(8,128)(2,1)S(1)}, bf16[4,256,256]{2,1,0:T(8,128)(2,1)S(1)}, u32[]{:S(2)}, u32[]{:S(2)}) collective-permute-start(bf16[4,256,256]{2,1,0:T(8,128)(2,1)S(1)} %shard_map.109.own_ref), channel_id=1, source_target_pairs={{0,1},{1,0},{2,3},{3,2},{4,5},{5,4},{6,7},{7,6},{8,9},{9,8},{10,11... | collective-permute-start | bytes 1572872 | tf_op jit(solution)/shard_map/ppermute | solution.py:31
  42.8 21.0 %collective-permute-start.2 = (bf16[544,512]{1,0:T(8,128)(2,1)S(1)}, bf16[544,512]{1,0:T(8,128)(2,1)S(1)}, u32[]{:S(2)}, u32[]{:S(2)}) collective-permute-start(bf16[544,512]{1,0:T(8,128)(2,1)S(1)} %collective-permute-done.1.refs_6_), channel_id=1, source_target_pairs={{0,2},{1,3},{2,0},{3,1},{4,6},{5,7},{6,4},{7,5},{8,10},{9,11},{10,... | collective-permute-start | bytes 1671176 | tf_op jit(solution)/shard_map/ppermute | solution.py:31
  42.9 20.9 %collective-permute-start.4 = (bf16[544,512]{1,0:T(8,128)(2,1)S(1)}, bf16[544,512]{1,0:T(8,128)(2,1)S(1)}, u32[]{:S(2)}, u32[]{:S(2)}) collective-permute-start(bf16[544,512]{1,0:T(8,128)(2,1)S(1)} %collective-permute-done.3.refs_5_), channel_id=1, source_target_pairs={{0,4},{1,5},{2,6},{3,7},{4,0},{5,1},{6,2},{7,3},{8,12},{9,13},{10,... | collective-permute-start | bytes 1671176 | tf_op jit(solution)/shard_map/ppermute | solution.py:31
  62.8 12.7 %copy-start.6 = (f32[256,256]{1,0:T(8,128)S(1)}, f32[256,256]{1,0:T(8,128)}, u32[]{:S(2)}) copy-start(f32[256,256]{1,0:T(8,128)} %b1_ref.1) | copy-start | bytes 786436
  62.9 12.7 %copy-start.10 = (f32[64,256]{1,0:T(8,128)S(1)}, f32[64,256]{1,0:T(8,128)}, u32[]{:S(2)}) copy-start(f32[64,256]{1,0:T(8,128)} %copy-done.9) | copy-start | bytes 196612
  62.9 12.7 %copy-start.14 = (bf16[1024,512]{1,0:T(8,128)(2,1)S(1)}, bf16[1024,512]{1,0:T(8,128)(2,1)}, u32[]{:S(2)}) copy-start(bf16[1024,512]{1,0:T(8,128)(2,1)} %copy-done.13) | copy-start | bytes 3145732
  70.4 5.2 %copy-start.12 = (s32[4,3]{1,0:T(4,128)S(1)}, s32[4,3]{1,0:T(4,128)}, u32[]{:S(2)}) copy-start(s32[4,3]{1,0:T(4,128)} %lists_ref.1) | copy-start | bytes 148
  70.4 9.0 %collective-permute-start.7 = (f32[1024,128]{1,0:T(8,128)S(1)}, f32[1024,128]{1,0:T(8,128)S(1)}, u32[]{:S(2)}, u32[]{:S(2)}) collective-permute-start(f32[1024,128]{1,0:T(8,128)S(1)} %get-tuple-element.16), channel_id=1, source_target_pairs={{0,1},{1,0},{2,3},{3,2},{4,5},{5,4},{6,7},{7,6},{8,9},{9,8},{10,11... | collective-permute-start | bytes 1572872 | tf_op jit(solution)/shard_map/ppermute | solution.py:31

commit v2 on v1

--- a/solution.py
+++ b/solution.py
@@ -32,9 +32,9 @@
 
 
 def call(kernel, out, n_smem, operands, scratch=(), flops=0, loose=0,
-         far_memory=False):
+         vmem=16):
     specs = [pl.BlockSpec(memory_space=SMEM)] * n_smem
-    specs += [pl.BlockSpec(memory_space=pltpu.MemorySpace.HBM if far_memory else pl.ANY)] * loose
+    specs += [pl.BlockSpec(memory_space=pl.ANY)] * loose
     specs += [pl.BlockSpec(memory_space=VMEM)] * (len(operands) - n_smem - loose)
     multi = isinstance(out, (list, tuple))
     return pl.pallas_call(
@@ -46,7 +46,7 @@
         else pl.BlockSpec(memory_space=VMEM),
         scratch_shapes=list(scratch),
         cost_estimate=pl.CostEstimate(flops=flops, bytes_accessed=0, transcendentals=0),
-        compiler_params=pltpu.CompilerParams(vmem_limit_bytes=40 * 2**20),
+        compiler_params=pltpu.CompilerParams(vmem_limit_bytes=vmem * 2**20),
     )(*operands)
 
 
@@ -113,13 +113,14 @@
         rest = inv - p0.astype(F32)
         p1 = rest.astype(BF16)
         p2 = (rest - p1.astype(F32)).astype(BF16)
-        wide = jnp.zeros((8, ref.shape[1] - half), BF16)
-        if wide.shape[1]:
-            p0, p1, p2 = (jnp.concatenate([p, wide], 1) for p in (p0, p1, p2))
-        ref[half : half + 8, :] = p0
-        ref[half + 8 : half + 16, :] = p1
-        ref[half + 16 : half + 24, :] = p2
-        ref[half + 24 : half + 32, :] = jnp.zeros_like(p0)
+        spot = lax.broadcasted_iota(jnp.int32, row.shape, 0)
+        parts = jnp.where(spot == 0, p0.astype(F32), jnp.where(spot == 1, p1.astype(F32), 0.0))
+        parts = jnp.where(spot == 2, p2.astype(F32), parts)
+        parts = jnp.concatenate([parts, jnp.zeros_like(parts)], 0)
+        if ref.shape[1] > half:
+            wide = jnp.zeros((16, ref.shape[1] - half), F32)
+            parts = jnp.concatenate([parts, wide], 1)
+        ref[half : half + 16, :] = parts.astype(BF16)
 
 
 def listed(lists_ref, row, value):
@@ -186,11 +187,8 @@
 
         @pl.when(active)
         def _():
-            inv_row = (
-                p_ref[k, half : half + 8, 0:half].astype(F32)
-                + p_ref[k, half + 8 : half + 16, 0:half].astype(F32)
-                + p_ref[k, half + 16 : half + 24, 0:half].astype(F32)
-            )[0:1, :]
+            parts = p_ref[k, half : half + 16, 0:half].astype(F32)
+            inv_row = jnp.sum(parts, axis=0, keepdims=True)
             weights = p_ref[k, 0:half, feats : feats + 2 * width]
             for i in range(size // tile):
                 at = pl.ds(i * tile, tile)
@@ -357,7 +355,7 @@
     pairs = [climb_pair, across(climb_pair, 1)]
 
     mate_pts = across(points, 1)
-    pack_shape = struct((size // 2 + 32, max(feats + 2 * width, size // 2)), BF16)
+    pack_shape = struct((size // 2 + 16, max(feats + 2 * width, size // 2)), BF16)
     pack_a, pack_b = call(
         pack_kernel, [pack_shape, pack_shape], 0, (points, rhs),
         [
@@ -365,11 +363,11 @@
             pltpu.VMEM((size, width), F32),
             pltpu.SemaphoreType.DMA((4,)),
         ],
+        flops=8 * 10**9,
         loose=2,
-        far_memory=True,
-    )
-    x_a, y_a = across(pack_a, 2), across(pack_a, 4)
-    x_b, y_b = across(pack_b, 2), across(pack_b, 4)
+    )
+    x_b, y_a = across(pack_b, 2), across(pack_a, 4)
+    x_a, y_b = across(pack_a, 2), across(pack_b, 4)
     d_a = across(y_a, 2)
     d_b = across(x_b, 4)
     masks = [NODE * m for m in range(1, nodes)]
@@ -411,7 +409,6 @@
             pltpu.SemaphoreType.DMA((3,)),
         ],
         loose=3,
-        far_memory=True,
         flops=2 * size * size * rank * 6,
     )
     strip = struct((rank // 2, width), F32)
@@ -433,8 +430,7 @@
     every_mate = across(every, 1)
 
     own = (pack_a, pack_b)
-    total = near((0, 0), ((0, 0), (0, 1)), own)
-    total = near((0, 0), ((1, 0), (1, 1)), own, total)
+    total = near((0, 0), ((0, 0), (0, 1), (1, 0), (1, 1)), own)
     jobs = [(t, k) for t in range(2) for k in range(4)]
     total = near((2, 2, 4, 4), jobs, (x_a, x_b, y_a, y_b), total)
     jobs = ((0, 0), (0, 1), (1, 0), (1, 1))

time: 80.6 us -> 77.7 us (0.964)
  Pallas kernels: 39.3 us -> 36.6 us
    pallas_call x12 -> x11, Pallas kernels: 39.3 us -> 36.6 us  [call(): pl.pallas_call(kernel, out_shape=out, in_specs=specs, out_specs=[pl.Block...]
    unnamed x33 -> x41, local copies, waits for them, and re-layouts: 5 us -> 5.03 us
  transfers between devices with their start and end apart: 20 -> 20, of which waited for: 5 -> 8; matrix products, arithmetic and copies ran while one was open for 0% -> 0% of each run, Pallas kernels for 47% -> 45%
where the time goes in v2:
time: 77.7 us; the launch traced here: 77.4 us
  Pallas kernels  36.6 us (47%)
  starting transfers between devices  20.2 us (26%)
  waiting for transfers between devices  15.3 us (20%)
  local copies, waits for them, and re-layouts  5.03 us (6%)
    pallas_call x11, Pallas kernels, call(): pl.pallas_call(kernel, out_shape=out, in_specs=specs, out_specs=[pl.Block...  36.6 us
    ppermute x20, starting transfers between devices, across(): return lax.ppermute(value, AXES, pairs)  20.2 us
    ppermute x20, waiting for transfers between devices, across(): return lax.ppermute(value, AXES, pairs)  15.3 us
    unnamed x41, local copies, waits for them, and re-layouts  5.03 us
  transfers between devices with their start and end apart: 20, of which 8 were waited for; matrix products, arithmetic and copies ran while one was open for 0% of the time, Pallas kernels for 45%

profile of v2, /device:TPU:9, one launch (start us, length us, event | category | flops | bytes accessed | tf_op | source)
XLA Modules:
  0.0 77.4 jit_solution(12544003023291989738)
XLA Ops:
  0.0 1.2 %collective-permute-start.10 = (f32[64,256]{1,0:T(8,128)}, f32[64,256]{1,0:T(8,128)S(1)}, u32[]{:S(2)}, u32[]{:S(2)}) collective-permute-start(f32[64,256]{1,0:T(8,128)} %refs_2_.9), channel_id=1, source_target_pairs={{0,2},{1,3},{2,0},{3,1},{4,6},{5,7},{6,4},{7,5},{8,10},{9,11},{10,... | collective-permute-start | bytes 196616 | tf_op jit(solution)/shard_map/ppermute | solution.py:31
  1.2 1.1 %collective-permute-start.11 = (f32[64,256]{1,0:T(8,128)}, f32[64,256]{1,0:T(8,128)S(1)}, u32[]{:S(2)}, u32[]{:S(2)}) collective-permute-start(f32[64,256]{1,0:T(8,128)} %refs_2_.9), channel_id=1, source_target_pairs={{0,3},{1,2},{2,1},{3,0},{4,7},{5,6},{6,5},{7,4},{8,11},{9,10},{10,... | collective-permute-start | bytes 196616 | tf_op jit(solution)/shard_map/ppermute | solution.py:31
  2.3 0.0 collective-permute-start.9
  2.3 0.5 collective-permute-start.8
  2.8 1.2 %copy-done.1 = f32[256,1024]{1,0:T(8,128)S(1)} copy-done((f32[256,1024]{1,0:T(8,128)S(1)}, f32[256,1024]{1,0:T(8,128)}, u32[]{:S(2)}) %copy-start.1) | copy-done | bytes 1048600
  4.0 1.0 %copy-done.2 = f32[1024,128]{1,0:T(8,128)S(1)} copy-done((f32[1024,128]{1,0:T(8,128)S(1)}, f32[1024,128]{1,0:T(8,128)}, u32[]{:S(2)}) %copy-start.2) | copy-done | bytes 524312
  5.1 0.9 %copy-done.5 = f32[256,256]{1,0:T(8,128)S(1)} copy-done((f32[256,256]{1,0:T(8,128)S(1)}, f32[256,256]{1,0:T(8,128)}, u32[]{:S(2)}) %copy-start.5) | copy-done | bytes 262168
  6.0 0.7 copy-done.15
  6.7 3.3 %shard_map.104 = (bf16[1024,512]{1,0:T(8,128)(2,1)S(1)}, f32[256,128]{1,0:T(8,128)S(1)}) custom-call(f32[256,1024]{1,0:T(8,128)S(1)} %copy-done.1, f32[1024,128]{1,0:T(8,128)S(1)} %copy-done.2, f32[256,256]{1,0:T(8,128)S(1)} %copy-done.5, s32[1,1024]{1,0:T(1,128)S(1)} %bitcast.2), custom_call_target="tpu_custom_call" | custom-call | flops 3221225472 | tf_op jit(solution)/shard_map/pallas_call | solution.py:40
  10.0 0.0 copy-start.17
  10.0 1.0 %copy-done.17 = bf16[1024,512]{1,0:T(8,128)(2,1)} copy-done((bf16[1024,512]{1,0:T(8,128)(2,1)}, bf16[1024,512]{1,0:T(8,128)(2,1)S(1)}, u32[]{:S(2)}) %copy-start.17) | copy-done | bytes 1048600
  11.0 0.0 collective-permute-done.10.refs_4_
  11.0 0.0 collective-permute-done.11.refs_5_
  11.0 0.0 copy-start.11
  11.0 0.0 collective-permute-done.9.refs_3_
  11.1 0.0 copy-start.13
  11.1 0.0 collective-permute-done.8.refs_1_
  11.1 0.0 copy-done.7
  11.1 0.0 copy-done.8
  11.1 0.0 copy-start
  11.1 0.8 %shard_map.105 = (f32[128,128]{1,0:T(8,128)S(1)}, f32[128,128]{1,0:T(8,128)S(1)}) custom-call(s32[1]{0:T(128)} %bitcast.refs_0_.flat_ref, f32[256,128]{1,0:T(8,128)S(1)} %get-tuple-element.17.part_ref, f32[128,256]{1,0:T(8,128)S(1)} %copy-done.7, f32[128,256]{1,0:T(8,128)S(1)} %collective-permute-done.8.refs_1_, f32[64,256]{1,0:T(8,128)S(1)} %copy-done.8, ...), custom_call_target="tpu_custom_call" | custom-call | flops 201326592 | tf_op jit(solution)/shard_map/pallas_call | solution.py:40
  11.9 0.0 copy-start.3
  11.9 0.1 collective-permute-start.12
  12.0 1.2 %collective-permute-done.12.got_ref = f32[128,128]{1,0:T(8,128)S(1)} collective-permute-done((f32[128,128]{1,0:T(8,128)S(1)}, f32[128,128]{1,0:T(8,128)S(1)}, u32[]{:S(2)}, u32[]{:S(2)}) %collective-permute-start.12) | collective-permute-done | bytes 65568 | tf_op jit(solution)/shard_map/ppermute | solution.py:31
  13.3 1.3 %collective-permute-start.13 = (bf16[160,256]{1,0:T(8,128)(2,1)S(1)}, bf16[160,256]{1,0:T(8,128)(2,1)S(1)}, u32[]{:S(2)}, u32[]{:S(2)}) collective-permute-start(bf16[160,256]{1,0:T(8,128)(2,1)S(1)} %shard_map.106.refs_0_), channel_id=1, source_target_pairs={{0,2},{1,3},{2,0},{3,1},{4,6},{5,7},{6,4},{7,5},{8,10},{9,11},{10,... | collective-permute-start | bytes 245768 | tf_op jit(solution)/shard_map/ppermute | solution.py:31
  14.6 1.2 %collective-permute-start.14 = (bf16[160,256]{1,0:T(8,128)(2,1)S(1)}, bf16[160,256]{1,0:T(8,128)(2,1)S(1)}, u32[]{:S(2)}, u32[]{:S(2)}) collective-permute-start(bf16[160,256]{1,0:T(8,128)(2,1)S(1)} %shard_map.106.refs_0_), channel_id=1, source_target_pairs={{0,4},{1,5},{2,6},{3,7},{4,0},{5,1},{6,2},{7,3},{8,12},{9,13},{10,... | collective-permute-start | bytes 245768 | tf_op jit(solution)/shard_map/ppermute | solution.py:31
  15.8 0.2 collective-permute-start.15
  16.0 1.0 %collective-permute-start = (bf16[1024,256]{1,0:T(8,128)(2,1)S(1)}, bf16[1024,256]{1,0:T(8,128)(2,1)S(1)}, u32[]{:S(2)}, u32[]{:S(2)}) collective-permute-start(bf16[1024,256]{1,0:T(8,128)(2,1)S(1)} %copy-done.4), channel_id=1, source_target_pairs={{0,1},{1,0},{2,3},{3,2},{4,5},{5,4},{6,7},{7,6},{8,9},{9,8},{10,11... | collective-permute-start | bytes 1572872 | tf_op jit(solution)/shard_map/ppermute | solution.py:31
  17.0 0.2 collective-permute-done.13.refs_1_
  17.2 0.7 collective-permute-done.14.refs_2_
  17.9 2.1 %collective-permute-done.15.refs_3_ = bf16[160,256]{1,0:T(8,128)(2,1)S(1)} collective-permute-done((bf16[160,256]{1,0:T(8,128)(2,1)S(1)}, bf16[160,256]{1,0:T(8,128)(2,1)S(1)}, u32[]{:S(2)}, u32[]{:S(2)}) %collective-permute-start.15) | collective-permute-done | bytes 81952 | tf_op jit(solution)/shard_map/ppermute | solution.py:31
  20.0 0.2 collective-permute-start.16
  20.3 2.3 %collective-permute-start.17 = (bf16[256,256]{1,0:T(8,128)(2,1)S(1)}, bf16[256,256]{1,0:T(8,128)(2,1)S(1)}, u32[]{:S(2)}, u32[]{:S(2)}) collective-permute-start(bf16[256,256]{1,0:T(8,128)(2,1)S(1)} %shard_map.107.refs_0_), channel_id=1, source_target_pairs={{0,16},{1,17},{2,18},{3,19},{4,20},{5,21},{6,22},{7,23},{8,24},{9,... | collective-permute-start | bytes 393224 | tf_op jit(solution)/shard_map/ppermute | solution.py:31
  22.6 0.2 collective-permute-start.18
  22.8 0.7 shard_map.100
  23.5 0.4 collective-permute-start.1
  23.9 0.1 copy.13.refs_1_
  24.0 0.0 collective-permute-done.16.refs_1_
  24.0 0.8 %collective-permute-start.5 = (bf16[528,512]{1,0:T(8,128)(2,1)S(1)}, bf16[528,512]{1,0:T(8,128)(2,1)S(1)}, u32[]{:S(2)}, u32[]{:S(2)}) collective-permute-start(bf16[528,512]{1,0:T(8,128)(2,1)S(1)} %get-tuple-element.13.refs_4_), channel_id=1, source_target_pairs={{0,2},{1,3},{2,0},{3,1},{4,6},{5,7},{6,4},{7,5},{8,10},{9,11},{10,... | collective-permute-start | bytes 1622024 | tf_op jit(solution)/shard_map/ppermute | solution.py:31
  24.8 2.0 %collective-permute-done.17.refs_2_ = bf16[256,256]{1,0:T(8,128)(2,1)S(1)} collective-permute-done((bf16[256,256]{1,0:T(8,128)(2,1)S(1)}, bf16[256,256]{1,0:T(8,128)(2,1)S(1)}, u32[]{:S(2)}, u32[]{:S(2)}) %collective-permute-start.17) | collective-permute-done | bytes 131104 | tf_op jit(solution)/shard_map/ppermute | solution.py:31
  26.8 1.5 %collective-permute-start.3 = (bf16[528,512]{1,0:T(8,128)(2,1)S(1)}, bf16[528,512]{1,0:T(8,128)(2,1)S(1)}, u32[]{:S(2)}, u32[]{:S(2)}) collective-permute-start(bf16[528,512]{1,0:T(8,128)(2,1)S(1)} %get-tuple-element.14.refs_5_), channel_id=1, source_target_pairs={{0,2},{1,3},{2,0},{3,1},{4,6},{5,7},{6,4},{7,5},{8,10},{9,11},{10,... | collective-permute-start | bytes 1622024 | tf_op jit(solution)/shard_map/ppermute | solution.py:31
  28.3 5.4 %collective-permute-done.18.refs_3_ = bf16[256,256]{1,0:T(8,128)(2,1)S(1)} collective-permute-done((bf16[256,256]{1,0:T(8,128)(2,1)S(1)}, bf16[256,256]{1,0:T(8,128)(2,1)S(1)}, u32[]{:S(2)}, u32[]{:S(2)}) %collective-permute-start.18) | collective-permute-done | bytes 131104 | tf_op jit(solution)/shard_map/ppermute | solution.py:31
  33.8 0.3 collective-permute-start.6
  34.1 0.0 collective-permute-done.refs_3_
  34.1 2.2 %collective-permute-start.19 = (bf16[4,256,256]{2,1,0:T(8,128)(2,1)S(1)}, bf16[4,256,256]{2,1,0:T(8,128)(2,1)S(1)}, u32[]{:S(2)}, u32[]{:S(2)}) collective-permute-start(bf16[4,256,256]{2,1,0:T(8,128)(2,1)S(1)} %shard_map.108.own_ref), channel_id=1, source_target_pairs={{0,1},{1,0},{2,3},{3,2},{4,5},{5,4},{6,7},{7,6},{8,9},{9,8},{10,11... | collective-permute-start | bytes 1572872 | tf_op jit(solution)/shard_map/ppermute | solution.py:31
  36.4 10.5 %shard_map.101.refs_8_ = f32[2,1024,128]{2,1,0:T(8,128)S(1)} custom-call(s32[1]{0:T(128)} %bitcast.refs_0_.flat_ref, s32[32,8]{1,0:T(8,128)S(1)} %copy.13.refs_1_, bf16[1024,256]{1,0:T(8,128)(2,1)S(1)} %copy-done.4, bf16[1024,256]{1,0:T(8,128)(2,1)S(1)} %collective-permute-done.refs_3_, bf16[528,512]{1,0:T(8,128)(2,1)S(1)} %get-tuple-element.13.refs_4_, ...), custom_call_target="tpu_custom_call" | custom-call | flops 17179869184 | tf_op jit(solution)/shard_map/pallas_call | solution.py:40
  46.8 0.0 collective-permute-done.1.refs_6_
  46.8 0.1 collective-permute-start.2
  46.9 0.0 collective-permute-done.3.refs_5_
  46.9 0.1 collective-permute-start.4
  47.0 0.0 collective-permute-done.5.refs_4_
  47.0 1.0 %collective-permute-done.6.refs_7_ = bf16[528,512]{1,0:T(8,128)(2,1)S(1)} collective-permute-done((bf16[528,512]{1,0:T(8,128)(2,1)S(1)}, bf16[528,512]{1,0:T(8,128)(2,1)S(1)}, u32[]{:S(2)}, u32[]{:S(2)}) %collective-permute-start.6) | collective-permute-done | bytes 540704 | tf_op jit(solution)/shard_map/ppermute | solution.py:31
  48.1 10.6 %shard_map.102.refs_6_ = f32[2,1024,128]{2,1,0:T(8,128)S(1)} custom-call(s32[1]{0:T(128)} %bitcast.refs_0_.flat_ref, s32[32,8]{1,0:T(8,128)S(1)} %copy.13.refs_1_, bf16[1024,256]{1,0:T(8,128)(2,1)S(1)} %copy-done.4, bf16[1024,256]{1,0:T(8,128)(2,1)S(1)} %collective-permute-done.refs_3_, bf16[528,512]{1,0:T(8,128)(2,1)S(1)} %collective-permute-done.5.refs_4_, ...), custom_call_target="tpu_custom_call" | custom-call | flops 34359738368 | tf_op jit(solution)/shard_map/pallas_call | solution.py:40
  58.7 0.0 copy-start.6
  58.7 0.0 copy-start.14
  58.7 2.5 %collective-permute-done.2.refs_4_ = bf16[528,512]{1,0:T(8,128)(2,1)S(1)} collective-permute-done((bf16[528,512]{1,0:T(8,128)(2,1)S(1)}, bf16[528,512]{1,0:T(8,128)(2,1)S(1)}, u32[]{:S(2)}, u32[]{:S(2)}) %collective-permute-start.2) | collective-permute-done | bytes 540704 | tf_op jit(solution)/shard_map/ppermute | solution.py:31
  61.2 0.0 collective-permute-done.4.refs_5_
  61.2 6.0 %shard_map.103 = (f32[1024,128]{1,0:T(8,128)S(1)}, f32[1024,128]{1,0:T(8,128)S(1)}) custom-call(s32[1]{0:T(128)} %bitcast.refs_0_.flat_ref, s32[32,8]{1,0:T(8,128)S(1)} %copy.13.refs_1_, bf16[1024,256]{1,0:T(8,128)(2,1)S(1)} %copy-done.4, bf16[1024,256]{1,0:T(8,128)(2,1)S(1)} %collective-permute-done.refs_3_, ...), custom_call_target="tpu_custom_call" | custom-call | flops 17179869184 | tf_op jit(solution)/shard_map/pallas_call | solution.py:40
  67.2 0.0 copy-start.16
  67.2 5.5 %collective-permute-start.7 = (f32[1024,128]{1,0:T(8,128)S(1)}, f32[1024,128]{1,0:T(8,128)S(1)}, u32[]{:S(2)}, u32[]{:S(2)}) collective-permute-start(f32[1024,128]{1,0:T(8,128)S(1)} %get-tuple-element.16), channel_id=1, source_target_pairs={{0,1},{1,0},{2,3},{3,2},{4,5},{5,4},{6,7},{7,6},{8,9},{9,8},{10,11... | collective-permute-start | bytes 1572872 | tf_op jit(solution)/shard_map/ppermute | solution.py:31
  72.7 0.0 collective-permute-done.19.mate_ref
  72.8 3.8 %shard_map.109.c_ref = f32[1024,128]{1,0:T(8,128)S(1)} custom-call(s32[1]{0:T(128)} %bitcast.refs_0_.flat_ref, s32[4,3]{1,0:T(4,128)S(1)} %copy-done.16, bf16[4,256,256]{2,1,0:T(8,128)(2,1)S(1)} %shard_map.108.own_ref, bf16[4,256,256]{2,1,0:T(8,128)(2,1)S(1)} %collective-permute-done.19.mate_ref, f32[256,256]{1,0:T(8,128)S(1)} %copy-done.6, ...), custom_call_target="tpu_custom_call" | custom-call | flops 1006632960 | tf_op jit(solution)/shard_map/pallas_call | solution.py:40
  76.5 0.0 collective-permute-done.7.b_ref
  76.5 0.9 %shard_map.110 = f32[1024,128]{1,0:T(8,128)} custom-call(f32[1024,128]{1,0:T(8,128)S(1)} %get-tuple-element.15.a_ref, f32[1024,128]{1,0:T(8,128)S(1)} %collective-permute-done.7.b_ref, f32[1024,128]{1,0:T(8,128)S(1)} %shard_map.109.c_ref), custom_call_target="tpu_custom_call" | custom-call | tf_op jit(solution)/shard_map/pallas_call | solution.py:40
  (28 shorter events, 0.1 us)
Async XLA Ops:
  0.0 11.0 %collective-permute-start.10 = (f32[64,256]{1,0:T(8,128)}, f32[64,256]{1,0:T(8,128)S(1)}, u32[]{:S(2)}, u32[]{:S(2)}) collective-permute-start(f32[64,256]{1,0:T(8,128)} %refs_2_.9), channel_id=1, source_target_pairs={{0,2},{1,3},{2,0},{3,1},{4,6},{5,7},{6,4},{7,5},{8,10},{9,11},{10,... | collective-permute-start | bytes 196616 | tf_op jit(solution)/shard_map/ppermute | solution.py:31
  1.2 9.8 %collective-permute-start.11 = (f32[64,256]{1,0:T(8,128)}, f32[64,256]{1,0:T(8,128)S(1)}, u32[]{:S(2)}, u32[]{:S(2)}) collective-permute-start(f32[64,256]{1,0:T(8,128)} %refs_2_.9), channel_id=1, source_target_pairs={{0,3},{1,2},{2,1},{3,0},{4,7},{5,6},{6,5},{7,4},{8,11},{9,10},{10,... | collective-permute-start | bytes 196616 | tf_op jit(solution)/shard_map/ppermute | solution.py:31
  2.3 8.7 %collective-permute-start.9 = (f32[64,256]{1,0:T(8,128)}, f32[64,256]{1,0:T(8,128)S(1)}, u32[]{:S(2)}, u32[]{:S(2)}) collective-permute-start(f32[64,256]{1,0:T(8,128)} %refs_2_.9), channel_id=1, source_target_pairs={{0,1},{1,0},{2,3},{3,2},{4,5},{5,4},{6,7},{7,6},{8,9},{9,8},{10,11... | collective-permute-start | bytes 196616 | tf_op jit(solution)/shard_map/ppermute | solution.py:31
  2.3 8.8 %collective-permute-start.8 = (f32[128,256]{1,0:T(8,128)}, f32[128,256]{1,0:T(8,128)S(1)}, u32[]{:S(2)}, u32[]{:S(2)}) collective-permute-start(f32[128,256]{1,0:T(8,128)} %refs_0_.3), channel_id=1, source_target_pairs={{0,1},{1,0},{2,3},{3,2},{4,5},{5,4},{6,7},{7,6},{8,9},{9,8},{10,11... | collective-permute-start | bytes 393224 | tf_op jit(solution)/shard_map/ppermute | solution.py:31
  2.8 1.2 %copy-start.1 = (f32[256,1024]{1,0:T(8,128)S(1)}, f32[256,1024]{1,0:T(8,128)}, u32[]{:S(2)}) copy-start(f32[256,1024]{1,0:T(8,128)} %basis_hbm.1) | copy-start | bytes 3145732
  4.0 1.0 %copy-start.2 = (f32[1024,128]{1,0:T(8,128)S(1)}, f32[1024,128]{1,0:T(8,128)}, u32[]{:S(2)}) copy-start(f32[1024,128]{1,0:T(8,128)} %w_hbm.3) | copy-start | bytes 1572868
  5.1 0.9 %copy-start.5 = (f32[256,256]{1,0:T(8,128)S(1)}, f32[256,256]{1,0:T(8,128)}, u32[]{:S(2)}) copy-start(f32[256,256]{1,0:T(8,128)} %b1_ref.1) | copy-start | bytes 786436
  6.0 0.7 copy-start.15
  6.7 4.4 %copy-start.7 = (f32[128,256]{1,0:T(8,128)S(1)}, f32[128,256]{1,0:T(8,128)}, u32[]{:S(2)}) copy-start(f32[128,256]{1,0:T(8,128)} %refs_0_.3) | copy-start | bytes 393220
  6.7 4.4 %copy-start.8 = (f32[64,256]{1,0:T(8,128)S(1)}, f32[64,256]{1,0:T(8,128)}, u32[]{:S(2)}) copy-start(f32[64,256]{1,0:T(8,128)} %refs_2_.9) | copy-start | bytes 196612
  10.0 1.0 %copy-start.17 = (bf16[1024,512]{1,0:T(8,128)(2,1)}, bf16[1024,512]{1,0:T(8,128)(2,1)S(1)}, u32[]{:S(2)}) copy-start(bf16[1024,512]{1,0:T(8,128)(2,1)S(1)} %get-tuple-element.20.refs_6_) | copy-start | bytes 3145732
  11.0 5.0 %copy-start.4 = (bf16[1024,256]{1,0:T(8,128)(2,1)S(1)}, bf16[1024,256]{1,0:T(8,128)(2,1)}, u32[]{:S(2)}) copy-start(bf16[1024,256]{1,0:T(8,128)(2,1)} %refs_2_.7) | copy-start | bytes 1572868
  11.0 0.9 %copy-start.9 = (f32[64,256]{1,0:T(8,128)}, f32[64,256]{1,0:T(8,128)S(1)}, u32[]{:S(2)}) copy-start(f32[64,256]{1,0:T(8,128)S(1)} %collective-permute-done.10.refs_4_) | copy-start | bytes 196612
  11.0 0.9 %copy-start.11 = (f32[64,256]{1,0:T(8,128)}, f32[64,256]{1,0:T(8,128)S(1)}, u32[]{:S(2)}) copy-start(f32[64,256]{1,0:T(8,128)S(1)} %collective-permute-done.11.refs_5_) | copy-start | bytes 196612
  11.1 0.9 %copy-start.13 = (f32[64,256]{1,0:T(8,128)}, f32[64,256]{1,0:T(8,128)S(1)}, u32[]{:S(2)}) copy-start(f32[64,256]{1,0:T(8,128)S(1)} %collective-permute-done.9.refs_3_) | copy-start | bytes 196612
  11.1 2.2 %copy-start = (bf16[32,256]{1,0:T(8,128)(2,1)S(1)}, bf16[32,256]{1,0:T(8,128)(2,1)}, u32[]{:S(2)}) copy-start(bf16[32,256]{1,0:T(8,128)(2,1)} %pts_ref.1) | copy-start | bytes 49156
  11.9 10.8 %copy-start.3 = (f32[1024,128]{1,0:T(8,128)S(1)}, f32[1024,128]{1,0:T(8,128)}, u32[]{:S(2)}) copy-start(f32[1024,128]{1,0:T(8,128)} %w_hbm.3) | copy-start | bytes 1572868
  11.9 1.3 %collective-permute-start.12 = (f32[128,128]{1,0:T(8,128)S(1)}, f32[128,128]{1,0:T(8,128)S(1)}, u32[]{:S(2)}, u32[]{:S(2)}) collective-permute-start(f32[128,128]{1,0:T(8,128)S(1)} %get-tuple-element.19), channel_id=1, source_target_pairs={{0,1},{1,0},{2,3},{3,2},{4,5},{5,4},{6,7},{7,6},{8,9},{9,8},{10,11... | collective-permute-start | bytes 196616 | tf_op jit(solution)/shard_map/ppermute | solution.py:31
  13.3 3.9 %collective-permute-start.13 = (bf16[160,256]{1,0:T(8,128)(2,1)S(1)}, bf16[160,256]{1,0:T(8,128)(2,1)S(1)}, u32[]{:S(2)}, u32[]{:S(2)}) collective-permute-start(bf16[160,256]{1,0:T(8,128)(2,1)S(1)} %shard_map.106.refs_0_), channel_id=1, source_target_pairs={{0,2},{1,3},{2,0},{3,1},{4,6},{5,7},{6,4},{7,5},{8,10},{9,11},{10,... | collective-permute-start | bytes 245768 | tf_op jit(solution)/shard_map/ppermute | solution.py:31
  14.6 3.3 %collective-permute-start.14 = (bf16[160,256]{1,0:T(8,128)(2,1)S(1)}, bf16[160,256]{1,0:T(8,128)(2,1)S(1)}, u32[]{:S(2)}, u32[]{:S(2)}) collective-permute-start(bf16[160,256]{1,0:T(8,128)(2,1)S(1)} %shard_map.106.refs_0_), channel_id=1, source_target_pairs={{0,4},{1,5},{2,6},{3,7},{4,0},{5,1},{6,2},{7,3},{8,12},{9,13},{10,... | collective-permute-start | bytes 245768 | tf_op jit(solution)/shard_map/ppermute | solution.py:31
  15.8 4.2 %collective-permute-start.15 = (bf16[160,256]{1,0:T(8,128)(2,1)S(1)}, bf16[160,256]{1,0:T(8,128)(2,1)S(1)}, u32[]{:S(2)}, u32[]{:S(2)}) collective-permute-start(bf16[160,256]{1,0:T(8,128)(2,1)S(1)} %shard_map.106.refs_0_), channel_id=1, source_target_pairs={{0,6},{1,7},{2,4},{3,5},{4,2},{5,3},{6,0},{7,1},{8,14},{9,15},{10,... | collective-permute-start | bytes 245768 | tf_op jit(solution)/shard_map/ppermute | solution.py:31
  16.0 18.1 %collective-permute-start = (bf16[1024,256]{1,0:T(8,128)(2,1)S(1)}, bf16[1024,256]{1,0:T(8,128)(2,1)S(1)}, u32[]{:S(2)}, u32[]{:S(2)}) collective-permute-start(bf16[1024,256]{1,0:T(8,128)(2,1)S(1)} %copy-done.4), channel_id=1, source_target_pairs={{0,1},{1,0},{2,3},{3,2},{4,5},{5,4},{6,7},{7,6},{8,9},{9,8},{10,11... | collective-permute-start | bytes 1572872 | tf_op jit(solution)/shard_map/ppermute | solution.py:31
  20.0 3.9 %collective-permute-start.16 = (bf16[256,256]{1,0:T(8,128)(2,1)S(1)}, bf16[256,256]{1,0:T(8,128)(2,1)S(1)}, u32[]{:S(2)}, u32[]{:S(2)}) collective-permute-start(bf16[256,256]{1,0:T(8,128)(2,1)S(1)} %shard_map.107.refs_0_), channel_id=1, source_target_pairs={{0,8},{1,9},{2,10},{3,11},{4,12},{5,13},{6,14},{7,15},{8,0},{9,1},... | collective-permute-start | bytes 393224 | tf_op jit(solution)/shard_map/ppermute | solution.py:31
  20.3 6.5 %collective-permute-start.17 = (bf16[256,256]{1,0:T(8,128)(2,1)S(1)}, bf16[256,256]{1,0:T(8,128)(2,1)S(1)}, u32[]{:S(2)}, u32[]{:S(2)}) collective-permute-start(bf16[256,256]{1,0:T(8,128)(2,1)S(1)} %shard_map.107.refs_0_), channel_id=1, source_target_pairs={{0,16},{1,17},{2,18},{3,19},{4,20},{5,21},{6,22},{7,23},{8,24},{9,... | collective-permute-start | bytes 393224 | tf_op jit(solution)/shard_map/ppermute | solution.py:31
  22.6 11.2 %collective-permute-start.18 = (bf16[256,256]{1,0:T(8,128)(2,1)S(1)}, bf16[256,256]{1,0:T(8,128)(2,1)S(1)}, u32[]{:S(2)}, u32[]{:S(2)}) collective-permute-start(bf16[256,256]{1,0:T(8,128)(2,1)S(1)} %shard_map.107.refs_0_), channel_id=1, source_target_pairs={{0,24},{1,25},{2,26},{3,27},{4,28},{5,29},{6,30},{7,31},{8,16},{9,... | collective-permute-start | bytes 393224 | tf_op jit(solution)/shard_map/ppermute | solution.py:31
  22.8 1.1 %copy-start.19 = (s32[32,8]{0,1:T(8,128)S(1)}, s32[32,8]{0,1:T(8,128)}, u32[]{:S(2)}) copy-start(s32[32,8]{0,1:T(8,128)} %param.18) | copy-start | bytes 3076
  23.5 23.3 %collective-permute-start.1 = (bf16[528,512]{1,0:T(8,128)(2,1)S(1)}, bf16[528,512]{1,0:T(8,128)(2,1)S(1)}, u32[]{:S(2)}, u32[]{:S(2)}) collective-permute-start(bf16[528,512]{1,0:T(8,128)(2,1)S(1)} %get-tuple-element.13.refs_4_), channel_id=1, source_target_pairs={{0,4},{1,5},{2,6},{3,7},{4,0},{5,1},{6,2},{7,3},{8,12},{9,13},{10,... | collective-permute-start | bytes 1622024 | tf_op jit(solution)/shard_map/ppermute | solution.py:31
  24.0 23.0 %collective-permute-start.5 = (bf16[528,512]{1,0:T(8,128)(2,1)S(1)}, bf16[528,512]{1,0:T(8,128)(2,1)S(1)}, u32[]{:S(2)}, u32[]{:S(2)}) collective-permute-start(bf16[528,512]{1,0:T(8,128)(2,1)S(1)} %get-tuple-element.13.refs_4_), channel_id=1, source_target_pairs={{0,2},{1,3},{2,0},{3,1},{4,6},{5,7},{6,4},{7,5},{8,10},{9,11},{10,... | collective-permute-start | bytes 1622024 | tf_op jit(solution)/shard_map/ppermute | solution.py:31
  26.8 20.1 %collective-permute-start.3 = (bf16[528,512]{1,0:T(8,128)(2,1)S(1)}, bf16[528,512]{1,0:T(8,128)(2,1)S(1)}, u32[]{:S(2)}, u32[]{:S(2)}) collective-permute-start(bf16[528,512]{1,0:T(8,128)(2,1)S(1)} %get-tuple-element.14.refs_5_), channel_id=1, source_target_pairs={{0,2},{1,3},{2,0},{3,1},{4,6},{5,7},{6,4},{7,5},{8,10},{9,11},{10,... | collective-permute-start | bytes 1622024 | tf_op jit(solution)/shard_map/ppermute | solution.py:31
  33.8 14.3 %collective-permute-start.6 = (bf16[528,512]{1,0:T(8,128)(2,1)S(1)}, bf16[528,512]{1,0:T(8,128)(2,1)S(1)}, u32[]{:S(2)}, u32[]{:S(2)}) collective-permute-start(bf16[528,512]{1,0:T(8,128)(2,1)S(1)} %get-tuple-element.14.refs_5_), channel_id=1, source_target_pairs={{0,4},{1,5},{2,6},{3,7},{4,0},{5,1},{6,2},{7,3},{8,12},{9,13},{10,... | collective-permute-start | bytes 1622024 | tf_op jit(solution)/shard_map/ppermute | solution.py:31
  34.1 38.6 %collective-permute-start.19 = (bf16[4,256,256]{2,1,0:T(8,128)(2,1)S(1)}, bf16[4,256,256]{2,1,0:T(8,128)(2,1)S(1)}, u32[]{:S(2)}, u32[]{:S(2)}) collective-permute-start(bf16[4,256,256]{2,1,0:T(8,128)(2,1)S(1)} %shard_map.108.own_ref), channel_id=1, source_target_pairs={{0,1},{1,0},{2,3},{3,2},{4,5},{5,4},{6,7},{7,6},{8,9},{9,8},{10,11... | collective-permute-start | bytes 1572872 | tf_op jit(solution)/shard_map/ppermute | solution.py:31
  46.8 14.4 %collective-permute-start.2 = (bf16[528,512]{1,0:T(8,128)(2,1)S(1)}, bf16[528,512]{1,0:T(8,128)(2,1)S(1)}, u32[]{:S(2)}, u32[]{:S(2)}) collective-permute-start(bf16[528,512]{1,0:T(8,128)(2,1)S(1)} %collective-permute-done.1.refs_6_), channel_id=1, source_target_pairs={{0,2},{1,3},{2,0},{3,1},{4,6},{5,7},{6,4},{7,5},{8,10},{9,11},{10,... | collective-permute-start | bytes 1622024 | tf_op jit(solution)/shard_map/ppermute | solution.py:31
  46.9 14.3 %collective-permute-start.4 = (bf16[528,512]{1,0:T(8,128)(2,1)S(1)}, bf16[528,512]{1,0:T(8,128)(2,1)S(1)}, u32[]{:S(2)}, u32[]{:S(2)}) collective-permute-start(bf16[528,512]{1,0:T(8,128)(2,1)S(1)} %collective-permute-done.3.refs_5_), channel_id=1, source_target_pairs={{0,4},{1,5},{2,6},{3,7},{4,0},{5,1},{6,2},{7,3},{8,12},{9,13},{10,... | collective-permute-start | bytes 1622024 | tf_op jit(solution)/shard_map/ppermute | solution.py:31
  58.7 14.1 %copy-start.6 = (f32[256,256]{1,0:T(8,128)S(1)}, f32[256,256]{1,0:T(8,128)}, u32[]{:S(2)}) copy-start(f32[256,256]{1,0:T(8,128)} %b1_ref.1) | copy-start | bytes 786436
  58.7 14.1 %copy-start.10 = (f32[64,256]{1,0:T(8,128)S(1)}, f32[64,256]{1,0:T(8,128)}, u32[]{:S(2)}) copy-start(f32[64,256]{1,0:T(8,128)} %copy-done.9) | copy-start | bytes 196612
  58.7 14.1 %copy-start.12 = (f32[64,256]{1,0:T(8,128)S(1)}, f32[64,256]{1,0:T(8,128)}, u32[]{:S(2)}) copy-start(f32[64,256]{1,0:T(8,128)} %copy-done.11) | copy-start | bytes 196612
  58.7 14.1 %copy-start.14 = (f32[64,256]{1,0:T(8,128)S(1)}, f32[64,256]{1,0:T(8,128)}, u32[]{:S(2)}) copy-start(f32[64,256]{1,0:T(8,128)} %copy-done.13) | copy-start | bytes 196612
  58.7 14.1 %copy-start.18 = (bf16[1024,512]{1,0:T(8,128)(2,1)S(1)}, bf16[1024,512]{1,0:T(8,128)(2,1)}, u32[]{:S(2)}) copy-start(bf16[1024,512]{1,0:T(8,128)(2,1)} %copy-done.17) | copy-start | bytes 3145732
  67.2 5.5 %copy-start.16 = (s32[4,3]{1,0:T(4,128)S(1)}, s32[4,3]{1,0:T(4,128)}, u32[]{:S(2)}) copy-start(s32[4,3]{1,0:T(4,128)} %lists_ref.1) | copy-start | bytes 148
  67.2 9.3 %collective-permute-start.7 = (f32[1024,128]{1,0:T(8,128)S(1)}, f32[1024,128]{1,0:T(8,128)S(1)}, u32[]{:S(2)}, u32[]{:S(2)}) collective-permute-start(f32[1024,128]{1,0:T(8,128)S(1)} %get-tuple-element.16), channel_id=1, source_target_pairs={{0,1},{1,0},{2,3},{3,2},{4,5},{5,4},{6,7},{7,6},{8,9},{9,8},{10,11... | collective-permute-start | bytes 1572872 | tf_op jit(solution)/shard_map/ppermute | solution.py:31
